TPU v7x, 32 devices: a whole 2x2x4 slice. The times are simulated.
32 devices in a mesh: gx: 4 (over x, core), gy: 8 (over z, y).
Axes of the slice: x: 2, y: 2, z: 4, core: 2. Of those that a mesh axis runs over, the one named last changes fastest.
Arguments:
- concentration: float32 [192, 5, 32768], P(('gx', 'gy')), may hold values from 0.05 to 3
- neighbours: int32 [192, 6], P(('gx', 'gy')), may hold values from -1 to 191, as said below
- source_slot: int32 [192], P(('gx', 'gy')), may hold values from -1 to 191, as said below
- mobility: float32 [5], replicated, may hold values from 0.3 to 2
- fermi_gain: float32 [5], replicated, may hold values from 0.3 to 3
- rates: float32 [5], replicated, may hold values from 0.05 to 0.5
Outputs:
- moved: float32 [192, 5, 32768], P(('gx', 'gy'))
Inputs may be any that keep to these rules, and one draw needn't show every extreme that they name: neighbours: each entry is -1 or a slot on the same device or on a device next to it along gx or along gy (same index on the other axis); every slot that source_slot names has neighbours that name only such slots that source_slot names too or -1. source_slot: each entry is -1 or a slot on the same device or on a device next to it along gx or along gy; no slot is named twice; only slots below 2 of a device are other than -1; at most 1 slots of one device name slots of one other device, and some device names exactly 1 of a neighbour's.
All inputs are finite; a program needn't handle non-finite values.
Results may differ from a plain program's by a relative error of at most 0.0003.
Values sent between devices are 32-bit elements; how exact they have to be, the bound alone decides.
No kernel may reach another device: no remote copies, remote signals or barrier semaphores. Data moves between devices by JAX's collectives and lax.ppermute only.
A program may use at most 192 MiB of HBM per device.

v0:
```python
import functools

import jax
import jax.numpy as jnp
from jax import lax
from jax.experimental import pallas as pl
from jax.experimental.pallas import tpu as pltpu
from jax.sharding import PartitionSpec as P


B = 32
SPECIES = 5
SWEEPS = 3
KEEP = 2
MOVE = 1
WORKING = KEEP - 1 + MOVE
SIDES = 6
TILES = B * B // 128
LAYER = (TILES, 128)
PAD = 2 * TILES


VMEM = pl.BlockSpec(memory_space=pltpu.VMEM)
SMEM = pl.BlockSpec(memory_space=pltpu.SMEM)
ANY = pl.BlockSpec(memory_space=pl.ANY)
F32 = jnp.float32
VMEM_LIMIT = 24 << 20


def iotas():
    sub = lax.broadcasted_iota(jnp.int32, LAYER, 0)
    lane = lax.broadcasted_iota(jnp.int32, LAYER, 1)
    return sub, lane


def raw_copy(c_ref, raw, sems, cap, s):
    return pltpu.make_async_copy(c_ref.at[s], raw.at[s, :, pl.ds(0, cap), :], sems.at[s])


def raw_rows(raw):
    return raw.reshape(SPECIES * B * TILES * 8, 128)


PER_X = TILES * 8
PER_S = B * PER_X


class Table:
    def __init__(self, cap, rows, devices):
        self.cap, self.rows, self.devices = cap, rows, devices
        self.width = -(-(1 + SIDES) * cap // 8) * 8
        self.scale = -(-(1 << 16) // cap)
        assert all((p * self.scale) >> 16 == p // cap for p in range(cap * devices))

    def gather(self, neighbours, source_slot):
        own = jnp.concatenate([source_slot, neighbours.reshape(-1)])
        own = jnp.pad(own, (0, self.width - own.shape[0]))
        sent = jnp.broadcast_to(own[None], (self.devices, self.width))
        return lax.all_to_all(sent, ("gx", "gy"), 0, 0, tiled=True).reshape(-1)

    def device(self, slot):
        return (slot * self.scale) >> 16

    def there(self, device):
        return jnp.clip(device, 0, self.devices - 1)

    def take(self, table, device, t):
        return table[self.there(device) * self.width + t]

    def local(self, slot, device):
        at = slot - device * self.cap
        return (at >= 0) & (at < self.cap), jnp.clip(at, 0, self.cap - 1)

    def need(self, table, slot, side):
        safe = jnp.maximum(slot, 0)
        home = self.device(safe)
        near = table[home * self.width + self.cap + (safe - home * self.cap) * SIDES + side]
        face = jnp.where(near < 0, side, side ^ 1)
        return jnp.where(slot < 0, -1, jnp.where(near < 0, slot, near)), face


def each_side(body):
    def step(f, carry):
        body(f)
        return carry

    lax.fori_loop(0, SIDES, step, 0)


def copy_face(dst, dst_at, src, src_at):
    for s in range(SPECIES):
        dst[dst_at, s] = src[src_at, s]


def picked(info, table, me, device):
    pick = jnp.int32(0)
    for t in range(WORKING):
        here, at = info.local(info.take(table, device, t), me)
        pick = jnp.where(here, at, pick)
    return pick


def pack_kernel(cap, c_ref, dense, faces, raw, sems):
    for s in range(SPECIES):
        raw_copy(c_ref, raw, sems, cap, s).start()
    rows = raw_rows(raw)
    _, lane = iotas()
    z = lane & (B - 1)
    quarter = lane // B

    def species(s, carry):
        raw_copy(c_ref, raw, sems, cap, s).wait()
        base = s * PER_S

        def slot(p, carry2):
            start = base + p
            z_first = z_last = None
            for x in range(B):
                v = rows[pl.ds(start + x * PER_X, TILES, stride=8), :]
                dense[p, s, x] = v
                a = v if x == 0 else pltpu.roll(v, x, 1)
                b = v if x == B - 1 else pltpu.roll(v, 128 + x - (B - 1), 1)
                z_first = a if x == 0 else jnp.where(z == x, a, z_first)
                z_last = b if x == 0 else jnp.where(z == x, b, z_last)
                if x == 0:
                    faces[p * SIDES + 0, s] = v
                if x == B - 1:
                    faces[p * SIDES + 1, s] = v
            y_first = y_last = None
            for j in range(4):
                a = rows[pl.ds(start + j * PER_X, TILES, stride=4 * PER_X), :]
                b = rows[pl.ds(start + j * PER_X + (TILES - 1) * 8, TILES, stride=4 * PER_X), :]
                a = a if j == 0 else pltpu.roll(a, j * B, 1)
                b = b if j == 3 else pltpu.roll(b, (j + 1) * B, 1)
                y_first = a if j == 0 else jnp.where(quarter == j, a, y_first)
                y_last = b if j == 0 else jnp.where(quarter == j, b, y_last)
            faces[p * SIDES + 2, s] = y_first
            faces[p * SIDES + 3, s] = y_last
            faces[p * SIDES + 4, s] = z_first
            faces[p * SIDES + 5, s] = z_last
            return carry2

        return lax.fori_loop(0, cap, slot, carry)

    lax.fori_loop(0, SPECIES, species, 0)


def copy_patches(pairs, dense):
    def layer(x, carry):
        for s in range(SPECIES):
            for number, out in pairs:
                out[s, x] = dense[number, s, x]
        return carry

    lax.fori_loop(0, B, layer, 0, unroll=4)


def first_kernel(info, me_ref, table, dense, to_yp, to_ym):
    me = me_ref[0]
    up, down = picked(info, table, me, me + 1), picked(info, table, me, me - 1)
    copy_patches(((up, to_yp), (down, to_ym)), dense)


def second_kernel(
    info, me_ref, table, dense, faces, to_xp, to_xm, to_x2p, to_x2m, to_y2p, to_y2m, patches
):
    me = me_ref[0]
    up, down = picked(info, table, me, me + info.rows), picked(info, table, me, me - info.rows)
    copy_patches(((up, to_xp), (down, to_xm)), dense)
    for t in range(WORKING):
        slot = info.take(table, me, t)
        kind = jnp.int32(-1)
        for c, device in enumerate((me, me - info.rows, me + info.rows, me - 1, me + 1)):
            kind = jnp.where((slot >= 0) & info.local(slot, device)[0], c, kind)
        patches[t] = kind
        patches[WORKING + t] = info.local(slot, me)[1]

    for step, out in ((info.rows, to_x2p), (-info.rows, to_x2m), (1, to_y2p), (-1, to_y2m)):
        for t in range(WORKING):
            slot = info.take(table, me + 2 * step, t)
            between, _ = info.local(slot, me + step)

            @pl.when(between)
            def _(slot=slot, out=out):
                @each_side
                def _(f):
                    near, face = info.need(table, slot, f)
                    here, at = info.local(near, me)
                    pl.when(here)(
                        functools.partial(copy_face, out, f, faces, at * SIDES + face)
                    )


def faces_kernel(info, me_ref, table, f_own, f_xm, f_xp, to_yp, to_ym, ghosts, plan):
    me = me_ref[0]
    shifts = ((0, f_own), (-info.rows, f_xm), (info.rows, f_xp))
    for step, out in ((1, to_yp), (-1, to_ym), (0, ghosts)):
        for t in range(WORKING):
            slot = info.take(table, me + step, t)

            @each_side
            def _(f, t=t, step=step, out=out, slot=slot):
                near, face = info.need(table, slot, f)
                at = t * SIDES + f
                for shift, src in shifts:
                    here, number = info.local(near, me + shift)
                    pl.when((near >= 0) & here)(
                        functools.partial(copy_face, out, at, src, number * SIDES + face)
                    )
                if step == 0:
                    home = info.device(jnp.maximum(near, 0))
                    column, my_column = home // info.rows, me // info.rows
                    row, my_row = home - column * info.rows, me - my_column * info.rows
                    beside = jnp.abs(column - my_column) < 2
                    kind, place = jnp.int32(0), at
                    kind = jnp.where(beside & (row == my_row - 1), 1, kind)
                    kind = jnp.where(beside & (row == my_row + 1), 2, kind)
                    for c, far in ((3, -2 * info.rows), (4, 2 * info.rows)):
                        kind = jnp.where(home == me + far, c, kind)
                    for c, far in ((5, -2), (6, 2)):
                        kind = jnp.where((column == my_column) & (row == my_row + far), c, kind)
                    place = jnp.where(kind > 2, f, place)
                    plan[at] = jnp.where(near >= 0, kind, 0)
                    plan[WORKING * SIDES + at] = place


def prepare_kernel(
    patches, mob, gain, rates, dense, p_xm, p_xp, p_ym, p_yp, grid, fixed, factor
):
    zero = jnp.zeros(LAYER, F32)

    def full(value):
        return jnp.full(LAYER, value, F32)

    flat, slope = [], []
    for s in range(SPECIES):
        m, g = full(mob[s]), full(gain[s])
        flat.append(m / (1.0 + g))
        slope.append(m * g / (1.0 + g))
    rate = [full(rates[i]) for i in range(5)]

    for t in range(WORKING):

        def prepare(load, t=t):
            def layer(x, carry):
                a, i, v, p, q = (load(s, x) for s in range(SPECIES))
                half = 0.5 * (a + p + q)
                electrons = half + jnp.sqrt(half * half + 1.0)
                pi = rate[0] * a * i - rate[1] * p
                pv = rate[2] * a * v - rate[3] * q
                re = rate[4] * (i * v - 1.0)
                source = (a - pi - pv, i - pi - re, v - pv - re, p + pi, q + pv)
                at = pl.multiple_of(x * PAD, 8)
                for s, value in enumerate((a, i, v, p, q)):
                    spread = flat[s] + slope[s] * electrons
                    inverse = 1.0 / (1.0 + 6.0 * spread)
                    grid[t, s, pl.ds(at, TILES), :] = zero
                    grid[t, s, pl.ds(at + TILES, TILES), :] = value
                    fixed[t, s, x] = source[s] * inverse
                    factor[t, s, x] = spread * inverse
                return carry

            lax.fori_loop(0, B, layer, 0, unroll=4)
            for s in range(SPECIES):
                grid[t, s, pl.ds(B * PAD, TILES), :] = zero

        kind = patches[t]
        pl.when(kind == 0)(
            functools.partial(prepare, lambda s, x, t=t: dense[patches[WORKING + t], s, x])
        )
        for c, src in ((1, p_xm), (2, p_xp), (3, p_ym), (4, p_yp)):
            pl.when(kind == c)(functools.partial(prepare, lambda s, x, src=src: src[s, x]))


def sweep_kernel(
    patches, plan, grid, fixed, factor, ghosts, g_ym, g_yp, g_xm, g_xp, g_y2m, g_y2p, blank,
    out_ref, ghost, mid, base, stage, sems,
):
    del blank
    sub, lane = iotas()
    z = lane & (B - 1)
    z_low, z_high = z == 0, z == B - 1
    y_low = (sub == 0) & (lane < B)
    y_high = (sub == TILES - 1) & (lane >= 128 - B)
    zero = jnp.zeros(LAYER, F32)
    stage_rows = raw_rows(stage)

    def clear_pad(i, carry):
        for a in range(2):
            mid[a, pl.ds(pl.multiple_of(i * PAD, 8), TILES), :] = zero
        return carry

    lax.fori_loop(0, B + 1, clear_pad, 0, unroll=3)

    def copy_out(s):
        return pltpu.make_async_copy(
            stage.at[s, :, pl.ds(0, WORKING), :],
            out_ref.at[s, :, pl.ds(0, WORKING), :],
            sems.at[s],
        )

    for t in range(WORKING):

        @each_side
        def _(f, t=t):
            kind = plan[t * SIDES + f]
            place = plan[WORKING * SIDES + t * SIDES + f]
            for c, src in enumerate((ghosts, g_ym, g_yp, g_xm, g_xp, g_y2m, g_y2p)):
                pl.when(kind == c)(functools.partial(copy_face, ghost, t * SIDES + f, src, place))

    def one_patch(t, s):
        at_side = t * SIDES
        y_first, y_last = ghost[at_side + 2, s], ghost[at_side + 3, s]
        z_first, z_last = ghost[at_side + 4, s], ghost[at_side + 5, s]
        firsts = [pltpu.roll(y_first, (128 - j * B) % 128, 1) if j else y_first for j in range(4)]
        lasts = [pltpu.roll(y_last, (3 - j) * B, 1) if j < 3 else y_last for j in range(4)]
        for x in range(B):
            zf = pltpu.roll(z_first, 128 - x, 1) if x else z_first
            zl = pltpu.roll(z_last, B - 1 - x, 1) if x < B - 1 else z_last
            i, j = x // 4, x % 4
            yf = pltpu.roll(firsts[j], TILES - i, 0) if i else firsts[j]
            yl = pltpu.roll(lasts[j], TILES - 1 - i, 0) if i < TILES - 1 else lasts[j]
            outer = jnp.where(z_low, zf, jnp.where(z_high, zl, zero))
            outer = outer + jnp.where(y_low, yf, jnp.where(y_high, yl, zero))
            if x == 0:
                outer = outer + ghost[at_side, s]
            if x == B - 1:
                outer = outer + ghost[at_side + 1, s]
            base[x] = fixed[t, s, x] + factor[t, s, x] * outer
        for sweep in range(SWEEPS):

            def load(row, sweep=sweep):
                if sweep == 0:
                    return grid[t, s, pl.ds(row, TILES), :]
                return mid[(sweep - 1) % 2, pl.ds(row, TILES), :]

            before = None
            here = load(TILES)
            for x in range(B):
                at = x * PAD + TILES
                after = load(at + PAD) if x < B - 1 else None
                total = pltpu.roll(jnp.where(lane >= 128 - B, load(at - 1), here), B, 1)
                total = total + pltpu.roll(jnp.where(lane < B, load(at + 1), here), 128 - B, 1)
                total = total + jnp.where(z_low, zero, pltpu.roll(here, 1, 1))
                total = total + jnp.where(z_high, zero, pltpu.roll(here, 127, 1))
                if before is not None:
                    total = total + before
                if after is not None:
                    total = total + after
                new = base[x] + factor[t, s, x] * total
                if sweep < SWEEPS - 1:
                    mid[sweep % 2, pl.ds(at, TILES), :] = new
                else:
                    stage_rows[pl.ds(s * PER_S + x * PER_X + t, TILES, stride=8), :] = new
                before, here = here, after

    def species(s, carry):
        for t in range(WORKING):
            live = patches[t] >= 0
            pl.when(live)(functools.partial(one_patch, t, s))

            @pl.when(jnp.logical_not(live))
            def _(t=t):
                for x in range(B):
                    stage_rows[pl.ds(s * PER_S + x * PER_X + t, TILES, stride=8), :] = zero

        copy_out(s).start()
        return carry

    lax.fori_loop(0, SPECIES, species, 0)
    for s in range(SPECIES):
        copy_out(s).wait()


def blank_kernel(cap, out_ref, zeros, sems):
    zeros[...] = jnp.zeros(zeros.shape, F32)

    def copy(s):
        return pltpu.make_async_copy(zeros.at[:, pl.ds(0, cap), :], out_ref.at[s], sems.at[s])

    for s in range(SPECIES):
        copy(s).start()
    for s in range(SPECIES):
        copy(s).wait()


def passed_along(x, axis, by):
    devices = lax.axis_size(axis)
    pairs = [(i, i + by) for i in range(devices) if 0 <= i + by < devices]
    return lax.ppermute(x, axis, pairs)


def both_ways(up, down, axis, by):
    return passed_along(up, axis, by), passed_along(down, axis, -by)


def call(kernel, out_shape, in_specs, out_specs, scratch=(), aliases=None):
    def run(*args):
        return pl.pallas_call(
            kernel,
            out_shape=out_shape,
            in_specs=in_specs,
            out_specs=out_specs,
            scratch_shapes=list(scratch),
            input_output_aliases=aliases or {},
            compiler_params=pltpu.CompilerParams(vmem_limit_bytes=VMEM_LIMIT),
        )(*args)

    return run


def shape(*dims, dtype=F32):
    return jax.ShapeDtypeStruct(dims, dtype)


def body(concentration, neighbours, source_slot, mobility, fermi_gain, rates):
    cap, species, cells = concentration.shape
    tiles = cells // 128
    rows, columns = lax.axis_size("gy"), lax.axis_size("gx")
    me = (lax.axis_index("gx") * rows + lax.axis_index("gy")).astype(jnp.int32)[None]
    info = Table(cap, rows, rows * columns)
    view = concentration.reshape(cap, species, tiles, 128).transpose(1, 2, 0, 3)
    table = info.gather(neighbours, source_slot)

    patch = shape(species, B, *LAYER)
    two_patches = shape(WORKING, species, B, *LAYER)
    all_sides = shape(WORKING * SIDES, species, *LAYER)
    one_patch = shape(SIDES, species, *LAYER)
    pack = call(
        functools.partial(pack_kernel, cap),
        (shape(cap, species, B, *LAYER), shape(cap * SIDES, species, *LAYER)),
        [ANY],
        (VMEM, VMEM),
        [pltpu.VMEM((species, tiles, 8, 128), F32), pltpu.SemaphoreType.DMA((species,))],
    )
    dense, faces = pack(view)
    blank = call(
        functools.partial(blank_kernel, cap),
        shape(species, tiles, cap, 128),
        [],
        ANY,
        [pltpu.VMEM((tiles, 8, 128), F32), pltpu.SemaphoreType.DMA((species,))],
    )()

    s_yp, s_ym = call(
        functools.partial(first_kernel, info), (patch,) * 2, [SMEM, SMEM, VMEM], (VMEM,) * 2
    )(me, table, dense)
    p_ym, p_yp = both_ways(s_yp, s_ym, "gy", 1)
    f_xm, f_xp = both_ways(faces, faces, "gx", 1)

    s_xp, s_xm, t_x2p, t_x2m, t_y2p, t_y2m, patches = call(
        functools.partial(second_kernel, info),
        (patch, patch) + (one_patch,) * 4 + (shape(2 * WORKING, dtype=jnp.int32),),
        [SMEM, SMEM, VMEM, VMEM],
        (VMEM,) * 6 + (SMEM,),
    )(me, table, dense, faces)
    p_xm, p_xp = both_ways(s_xp, s_xm, "gx", 1)

    t_yp, t_ym, ghosts, plan = call(
        functools.partial(faces_kernel, info),
        (all_sides,) * 3 + (shape(2 * WORKING * SIDES, dtype=jnp.int32),),
        [SMEM] * 2 + [VMEM] * 3,
        (VMEM,) * 3 + (SMEM,),
    )(me, table, faces, f_xm, f_xp)
    g_ym, g_yp = both_ways(t_yp, t_ym, "gy", 1)
    g_y2m, g_y2p = both_ways(t_y2p, t_y2m, "gy", 2)
    g_x2m, g_x2p = both_ways(t_x2p, t_x2m, "gx", 2)

    padded = shape(WORKING, species, B * PAD + TILES, 128)
    grid, fixed, factor = call(
        prepare_kernel, (padded, two_patches, two_patches), [SMEM] * 4 + [VMEM] * 5, (VMEM,) * 3
    )(patches, mobility, fermi_gain, rates, dense, p_xm, p_xp, p_ym, p_yp)

    moved = call(
        sweep_kernel,
        shape(species, tiles, cap, 128),
        [SMEM] * 2 + [VMEM] * 10 + [ANY],
        ANY,
        [
            pltpu.VMEM((WORKING * SIDES, species, *LAYER), F32),
            pltpu.VMEM((2, B * PAD + TILES, 128), F32),
            pltpu.VMEM((B, *LAYER), F32),
            pltpu.VMEM((species, tiles, 8, 128), F32),
            pltpu.SemaphoreType.DMA((species,)),
        ],
        {12: 0},
    )(patches, plan, grid, fixed, factor, ghosts, g_ym, g_yp, g_x2m, g_x2p, g_y2m, g_y2p, blank)
    return moved.transpose(2, 0, 1, 3).reshape(cap, species, cells)


def solution(mesh):
    placed = (P(("gx", "gy"), None, None), P(("gx", "gy"), None), P(("gx", "gy")), P(), P(), P())
    return jax.shard_map(
        body, mesh=mesh, in_specs=placed, out_specs=P(("gx", "gy"), None, None), check_vma=False
    )
```

profile of v0, /device:TPU:6, one launch (start us, length us, event | category | flops | bytes accessed | tf_op | source)
XLA Modules:
  0.0 92.7 jit_solution(5546854464094808600)
XLA Ops:
  0.0 2.5 %copy-done.3 = f32[6,5,32768]{2,0,1:T(8,128)S(1)} copy-done((f32[6,5,32768]{2,0,1:T(8,128)S(1)}, f32[6,5,32768]{2,0,1:T(8,128)}, u32[]{:S(2)}) %copy-start.3) | copy-done | bytes 3932184
  2.5 4.8 %shard_map.64 = (f32[6,5,32,8,128]{4,3,2,1,0:T(8,128)S(1)}, f32[36,5,8,128]{3,2,1,0:T(8,128)S(1)}) custom-call(f32[5,256,6,128]{3,2,1,0:T(8,128)S(1)} %bitcast.7), custom_call_target="tpu_custom_call" | custom-call | tf_op jit(solution)/shard_map/pallas_call | solution.py:399
  7.3 0.0 copy-start
  7.3 1.9 %copy-done = f32[6,5,32,8,128]{4,3,2,1,0:T(8,128)} copy-done((f32[6,5,32,8,128]{4,3,2,1,0:T(8,128)}, f32[6,5,32,8,128]{4,3,2,1,0:T(8,128)S(1)}, u32[]{:S(2)}) %copy-start) | copy-done | bytes 3932184
  9.2 1.9 %collective-permute-start.1 = (f32[36,5,8,128]{3,2,1,0:T(8,128)S(1)}, f32[36,5,8,128]{3,2,1,0:T(8,128)S(1)}, u32[]{:S(2)}, u32[]{:S(2)}) collective-permute-start(f32[36,5,8,128]{3,2,1,0:T(8,128)S(1)} %get-tuple-element.24.faces.f_own), channel_id=1, source_target_pairs={{8,0},{16,8},{24,16},{9,1},{17,9},{25,17},{10,2},{18,10},{26,18},{... | collective-permute-start | bytes 2211848 | tf_op jit(solution)/shard_map/ppermute | solution.py:390
  11.1 2.4 %collective-permute-start = (f32[36,5,8,128]{3,2,1,0:T(8,128)S(1)}, f32[36,5,8,128]{3,2,1,0:T(8,128)S(1)}, u32[]{:S(2)}, u32[]{:S(2)}) collective-permute-start(f32[36,5,8,128]{3,2,1,0:T(8,128)S(1)} %get-tuple-element.24.faces.f_own), channel_id=1, source_target_pairs={{0,8},{8,16},{16,24},{1,9},{9,17},{17,25},{2,10},{10,18},{18,26},{... | collective-permute-start | bytes 2211848 | tf_op jit(solution)/shard_map/ppermute | solution.py:390
  13.5 0.0 copy-done.7
  13.5 0.1 reshape.19
  13.6 0.0 copy-done.8
  13.6 0.1 pad_add_fusion
  13.7 0.6 broadcast_in_dim.10
  14.3 6.1 %all-to-all-start = ((s32[32,1,48]{2,1,0:T(1,128)}), s32[32,1,48]{2,1,0:T(1,128)S(1)}, u32[]{:S(2)}, u32[]{:S(2)}) async-start(s32[32,1,48]{2,1,0:T(1,128)} %broadcast_in_dim.10), calls=%async_computation | async-start | bytes 32768 | tf_op jit(solution)/shard_map/all_to_all | solution.py:59
  20.4 5.0 %all-to-all-done = s32[32,1,48]{2,1,0:T(1,128)S(1)} async-done(((s32[32,1,48]{2,1,0:T(1,128)}), s32[32,1,48]{2,1,0:T(1,128)S(1)}, u32[]{:S(2)}, u32[]{:S(2)}) %all-to-all-start) | async-done | bytes 6176 | tf_op jit(solution)/shard_map/all_to_all | solution.py:59
  25.4 0.5 broadcast.8
  26.0 0.7 reduce.3
  26.6 0.1 reshape.20.table
  26.7 2.1 %copy-done.1 = f32[6,5,32,8,128]{4,3,2,1,0:T(8,128)S(1)} copy-done((f32[6,5,32,8,128]{4,3,2,1,0:T(8,128)S(1)}, f32[6,5,32,8,128]{4,3,2,1,0:T(8,128)}, u32[]{:S(2)}) %copy-start.1) | copy-done | bytes 3932184
  28.8 1.6 %shard_map.65 = (f32[5,32,8,128]{3,2,1,0:T(8,128)S(1)}, f32[5,32,8,128]{3,2,1,0:T(8,128)S(1)}, f32[6,5,8,128]{3,2,1,0:T(8,128)S(1)}, f32[6,5,8,128]{3,2,1,0:T(8,...) custom-call(s32[1]{0:T(128)} %bitcast.me_ref, s32[1536]{0:T(1024)S(1)} %reshape.20.table, ...), custom_call_target="tpu_custom_call" | custom-call | tf_op jit(solution)/shard_map/pallas_call | solution.py:399
  30.5 1.9 %collective-permute-start.2 = (f32[5,32,8,128]{3,2,1,0:T(8,128)S(1)}, f32[5,32,8,128]{3,2,1,0:T(8,128)S(1)}, u32[]{:S(2)}, u32[]{:S(2)}) collective-permute-start(f32[5,32,8,128]{3,2,1,0:T(8,128)S(1)} %get-tuple-element.27), channel_id=1, source_target_pairs={{0,8},{8,16},{16,24},{1,9},{9,17},{17,25},{2,10},{10,18},{18,26},{... | collective-permute-start | bytes 1966088 | tf_op jit(solution)/shard_map/ppermute | solution.py:390
  32.4 3.6 %collective-permute-start.3 = (f32[5,32,8,128]{3,2,1,0:T(8,128)S(1)}, f32[5,32,8,128]{3,2,1,0:T(8,128)S(1)}, u32[]{:S(2)}, u32[]{:S(2)}) collective-permute-start(f32[5,32,8,128]{3,2,1,0:T(8,128)S(1)} %get-tuple-element.28), channel_id=1, source_target_pairs={{8,0},{16,8},{24,16},{9,1},{17,9},{25,17},{10,2},{18,10},{26,18},{... | collective-permute-start | bytes 1966088 | tf_op jit(solution)/shard_map/ppermute | solution.py:390
  36.0 0.8 shard_map.67
  36.8 0.0 copy-start.4
  36.8 0.0 copy-start.5
  36.8 0.0 copy-start.6
  36.9 3.4 %collective-permute-start.4 = (f32[5,32,8,128]{3,2,1,0:T(8,128)S(1)}, f32[5,32,8,128]{3,2,1,0:T(8,128)S(1)}, u32[]{:S(2)}, u32[]{:S(2)}) collective-permute-start(f32[5,32,8,128]{3,2,1,0:T(8,128)S(1)} %get-tuple-element.29), channel_id=1, source_target_pairs={{0,1},{1,2},{2,3},{3,4},{4,5},{5,6},{6,7},{8,9},{9,10},{10,11},{11... | collective-permute-start | bytes 1966088 | tf_op jit(solution)/shard_map/ppermute | solution.py:390
  40.3 0.0 collective-permute-done.1.f_xp
  40.3 2.7 %collective-permute-start.5 = (f32[5,32,8,128]{3,2,1,0:T(8,128)S(1)}, f32[5,32,8,128]{3,2,1,0:T(8,128)S(1)}, u32[]{:S(2)}, u32[]{:S(2)}) collective-permute-start(f32[5,32,8,128]{3,2,1,0:T(8,128)S(1)} %get-tuple-element.30), channel_id=1, source_target_pairs={{1,0},{2,1},{3,2},{4,3},{5,4},{6,5},{7,6},{9,8},{10,9},{11,10},{12... | collective-permute-start | bytes 1966088 | tf_op jit(solution)/shard_map/ppermute | solution.py:390
  43.0 0.0 collective-permute-done.f_xm
  43.0 1.3 %collective-permute-start.8 = (f32[6,5,8,128]{3,2,1,0:T(8,128)S(1)}, f32[6,5,8,128]{3,2,1,0:T(8,128)S(1)}, u32[]{:S(2)}, u32[]{:S(2)}) collective-permute-start(f32[6,5,8,128]{3,2,1,0:T(8,128)S(1)} %get-tuple-element.37), channel_id=1, source_target_pairs={{0,16},{8,24},{1,17},{9,25},{2,18},{10,26},{3,19},{11,27},{4,20},{... | collective-permute-start | bytes 368648 | tf_op jit(solution)/shard_map/ppermute | solution.py:390
  44.3 3.1 %shard_map.66 = (f32[12,5,8,128]{3,2,1,0:T(8,128)S(1)}, f32[12,5,8,128]{3,2,1,0:T(8,128)S(1)}, f32[12,5,8,128]{3,2,1,0:T(8,128)S(1)}, s32[24]{0:T(128)S(1)}) custom-call(s32[1]{0:T(128)} %bitcast.me_ref, s32[1536]{0:T(1024)S(1)} %reshape.20.table, f32[36,5,8,128]{3,2,1,0:T(8,128)S(1)} %get-tuple-element.24.faces.f_own, ...), custom_call_target="tpu_custom_call" | custom-call | tf_op jit(solution)/shard_map/pallas_call | solution.py:399
  47.5 2.3 %collective-permute-done.8.g_xm = f32[6,5,8,128]{3,2,1,0:T(8,128)S(1)} collective-permute-done((f32[6,5,8,128]{3,2,1,0:T(8,128)S(1)}, f32[6,5,8,128]{3,2,1,0:T(8,128)S(1)}, u32[]{:S(2)}, u32[]{:S(2)}) %collective-permute-start.8) | collective-permute-done | bytes 122912 | tf_op jit(solution)/shard_map/ppermute | solution.py:390
  49.8 4.0 %collective-permute-start.6 = (f32[12,5,8,128]{3,2,1,0:T(8,128)S(1)}, f32[12,5,8,128]{3,2,1,0:T(8,128)S(1)}, u32[]{:S(2)}, u32[]{:S(2)}) collective-permute-start(f32[12,5,8,128]{3,2,1,0:T(8,128)S(1)} %get-tuple-element.35), channel_id=1, source_target_pairs={{0,1},{1,2},{2,3},{3,4},{4,5},{5,6},{6,7},{8,9},{9,10},{10,11},{11... | collective-permute-start | bytes 737288 | tf_op jit(solution)/shard_map/ppermute | solution.py:390
  53.8 0.0 collective-permute-done.2.p_xm
  53.8 1.9 %collective-permute-start.7 = (f32[12,5,8,128]{3,2,1,0:T(8,128)S(1)}, f32[12,5,8,128]{3,2,1,0:T(8,128)S(1)}, u32[]{:S(2)}, u32[]{:S(2)}) collective-permute-start(f32[12,5,8,128]{3,2,1,0:T(8,128)S(1)} %get-tuple-element.36), channel_id=1, source_target_pairs={{1,0},{2,1},{3,2},{4,3},{5,4},{6,5},{7,6},{9,8},{10,9},{11,10},{12... | collective-permute-start | bytes 737288 | tf_op jit(solution)/shard_map/ppermute | solution.py:390
  55.7 0.0 collective-permute-done.3.p_xp
  55.8 2.2 %collective-permute-start.9 = (f32[6,5,8,128]{3,2,1,0:T(8,128)S(1)}, f32[6,5,8,128]{3,2,1,0:T(8,128)S(1)}, u32[]{:S(2)}, u32[]{:S(2)}) collective-permute-start(f32[6,5,8,128]{3,2,1,0:T(8,128)S(1)} %get-tuple-element.38), channel_id=1, source_target_pairs={{16,0},{24,8},{17,1},{25,9},{18,2},{26,10},{19,3},{27,11},{20,4},{... | collective-permute-start | bytes 368648 | tf_op jit(solution)/shard_map/ppermute | solution.py:390
  58.0 17.9 %collective-permute-done.4.p_ym = f32[5,32,8,128]{3,2,1,0:T(8,128)S(1)} collective-permute-done((f32[5,32,8,128]{3,2,1,0:T(8,128)S(1)}, f32[5,32,8,128]{3,2,1,0:T(8,128)S(1)}, u32[]{:S(2)}, u32[]{:S(2)}) %collective-permute-start.4) | collective-permute-done | bytes 655392 | tf_op jit(solution)/shard_map/ppermute | solution.py:390
  75.9 2.4 %collective-permute-start.10 = (f32[6,5,8,128]{3,2,1,0:T(8,128)S(1)}, f32[6,5,8,128]{3,2,1,0:T(8,128)S(1)}, u32[]{:S(2)}, u32[]{:S(2)}) collective-permute-start(f32[6,5,8,128]{3,2,1,0:T(8,128)S(1)} %get-tuple-element.39), channel_id=1, source_target_pairs={{0,2},{1,3},{2,4},{3,5},{4,6},{5,7},{8,10},{9,11},{10,12},{11,13},... | collective-permute-start | bytes 368648 | tf_op jit(solution)/shard_map/ppermute | solution.py:390
  78.4 0.0 collective-permute-done.5.p_yp
  78.4 1.3 %collective-permute-start.11 = (f32[6,5,8,128]{3,2,1,0:T(8,128)S(1)}, f32[6,5,8,128]{3,2,1,0:T(8,128)S(1)}, u32[]{:S(2)}, u32[]{:S(2)}) collective-permute-start(f32[6,5,8,128]{3,2,1,0:T(8,128)S(1)} %get-tuple-element.40), channel_id=1, source_target_pairs={{2,0},{3,1},{4,2},{5,3},{6,4},{7,5},{10,8},{11,9},{12,10},{13,11},... | collective-permute-start | bytes 368648 | tf_op jit(solution)/shard_map/ppermute | solution.py:390
  79.7 2.0 %shard_map.69.blank = f32[5,256,6,128]{3,2,1,0:T(8,128)} custom-call(), custom_call_target="tpu_custom_call" | custom-call | tf_op jit(solution)/shard_map/pallas_call | solution.py:399
  81.8 1.4 %shard_map.68 = (f32[2,5,520,128]{3,2,1,0:T(8,128)S(1)}, f32[2,5,32,8,128]{4,3,2,1,0:T(8,128)S(1)}, f32[2,5,32,8,128]{4,3,2,1,0:T(8,128)S(1)}) custom-call(s32[4]{0:T(128)S(1)} %get-tuple-element.25.patches, f32[5]{0:T(128)S(1)} %copy-done.4, f32[5]{0:T(128)S(1)} %copy-done.5, f32[5]{0:T(128)S(1)} %copy-done.6, f32[6,5,32,8,128]{4,3,2,1,0:T(8,128)S(1)} %copy-done.2, ...), custom_call_target="tpu_custom_call" | custom-call | tf_op jit(solution)/shard_map/pallas_call | solution.py:399
  83.2 0.0 collective-permute-done.9.g_xp
  83.2 0.0 collective-permute-done.10.g_y2m
  83.2 1.9 %collective-permute-done.11.g_y2p = f32[6,5,8,128]{3,2,1,0:T(8,128)S(1)} collective-permute-done((f32[6,5,8,128]{3,2,1,0:T(8,128)S(1)}, f32[6,5,8,128]{3,2,1,0:T(8,128)S(1)}, u32[]{:S(2)}, u32[]{:S(2)}) %collective-permute-start.11) | collective-permute-done | bytes 122912 | tf_op jit(solution)/shard_map/ppermute | solution.py:390
  85.2 0.0 collective-permute-done.6.g_ym
  85.2 0.0 collective-permute-done.7.g_yp
  85.2 7.5 %shard_map.70 = f32[5,256,6,128]{3,2,1,0:T(8,128)} custom-call(s32[4]{0:T(128)S(1)} %get-tuple-element.25.patches, s32[24]{0:T(128)S(1)} %get-tuple-element.26.plan, f32[2,5,520,128]{3,2,1,0:T(8,128)S(1)} %get-tuple-element.31.grid, f32[2,5,32,8,128]{4,3,2,1,0:T(8,128)S(1)} %get-tuple-element.32.fixed, ...), custom_call_target="tpu_custom_call", output_to_operand_aliasing={{}: (12, {})} | custom-call | tf_op jit(solution)/shard_map/pallas_call | solution.py:399
  (10 shorter events, 0.0 us)
Async XLA Ops:
  0.0 13.6 %copy-start.8 = (s32[6]{0:T(128)S(1)}, s32[6]{0:T(128)}, u32[]{:S(2)}) copy-start(s32[6]{0:T(128)} %param.8) | copy-start | bytes 76
  0.0 2.5 %copy-start.3 = (f32[6,5,32768]{2,0,1:T(8,128)S(1)}, f32[6,5,32768]{2,0,1:T(8,128)}, u32[]{:S(2)}) copy-start(f32[6,5,32768]{2,0,1:T(8,128)} %param.6) | copy-start | bytes 11796484
  2.5 11.0 %copy-start.7 = (s32[6,6]{1,0:T(8,128)S(1)}, s32[6,6]{1,0:T(8,128)}, u32[]{:S(2)}) copy-start(s32[6,6]{1,0:T(8,128)} %param.7) | copy-start | bytes 436
  7.3 1.9 %copy-start = (f32[6,5,32,8,128]{4,3,2,1,0:T(8,128)}, f32[6,5,32,8,128]{4,3,2,1,0:T(8,128)S(1)}, u32[]{:S(2)}) copy-start(f32[6,5,32,8,128]{4,3,2,1,0:T(8,128)S(1)} %get-tuple-element.23.dense) | copy-start | bytes 11796484
  9.2 31.1 %collective-permute-start.1 = (f32[36,5,8,128]{3,2,1,0:T(8,128)S(1)}, f32[36,5,8,128]{3,2,1,0:T(8,128)S(1)}, u32[]{:S(2)}, u32[]{:S(2)}) collective-permute-start(f32[36,5,8,128]{3,2,1,0:T(8,128)S(1)} %get-tuple-element.24.faces.f_own), channel_id=1, source_target_pairs={{8,0},{16,8},{24,16},{9,1},{17,9},{25,17},{10,2},{18,10},{26,18},{... | collective-permute-start | bytes 2211848 | tf_op jit(solution)/shard_map/ppermute | solution.py:390
  11.1 32.0 %collective-permute-start = (f32[36,5,8,128]{3,2,1,0:T(8,128)S(1)}, f32[36,5,8,128]{3,2,1,0:T(8,128)S(1)}, u32[]{:S(2)}, u32[]{:S(2)}) collective-permute-start(f32[36,5,8,128]{3,2,1,0:T(8,128)S(1)} %get-tuple-element.24.faces.f_own), channel_id=1, source_target_pairs={{0,8},{8,16},{16,24},{1,9},{9,17},{17,25},{2,10},{10,18},{18,26},{... | collective-permute-start | bytes 2211848 | tf_op jit(solution)/shard_map/ppermute | solution.py:390
  14.3 11.1 %all-to-all-start = ((s32[32,1,48]{2,1,0:T(1,128)}), s32[32,1,48]{2,1,0:T(1,128)S(1)}, u32[]{:S(2)}, u32[]{:S(2)}) async-start(s32[32,1,48]{2,1,0:T(1,128)} %broadcast_in_dim.10), calls=%async_computation | async-start | bytes 32768 | tf_op jit(solution)/shard_map/all_to_all | solution.py:59
  26.7 2.1 %copy-start.1 = (f32[6,5,32,8,128]{4,3,2,1,0:T(8,128)S(1)}, f32[6,5,32,8,128]{4,3,2,1,0:T(8,128)}, u32[]{:S(2)}) copy-start(f32[6,5,32,8,128]{4,3,2,1,0:T(8,128)} %copy-done) | copy-start | bytes 11796484
  30.5 23.3 %collective-permute-start.2 = (f32[5,32,8,128]{3,2,1,0:T(8,128)S(1)}, f32[5,32,8,128]{3,2,1,0:T(8,128)S(1)}, u32[]{:S(2)}, u32[]{:S(2)}) collective-permute-start(f32[5,32,8,128]{3,2,1,0:T(8,128)S(1)} %get-tuple-element.27), channel_id=1, source_target_pairs={{0,8},{8,16},{16,24},{1,9},{9,17},{17,25},{2,10},{10,18},{18,26},{... | collective-permute-start | bytes 1966088 | tf_op jit(solution)/shard_map/ppermute | solution.py:390
  32.4 23.4 %collective-permute-start.3 = (f32[5,32,8,128]{3,2,1,0:T(8,128)S(1)}, f32[5,32,8,128]{3,2,1,0:T(8,128)S(1)}, u32[]{:S(2)}, u32[]{:S(2)}) collective-permute-start(f32[5,32,8,128]{3,2,1,0:T(8,128)S(1)} %get-tuple-element.28), channel_id=1, source_target_pairs={{8,0},{16,8},{24,16},{9,1},{17,9},{25,17},{10,2},{18,10},{26,18},{... | collective-permute-start | bytes 1966088 | tf_op jit(solution)/shard_map/ppermute | solution.py:390
  36.8 44.9 %copy-start.2 = (f32[6,5,32,8,128]{4,3,2,1,0:T(8,128)S(1)}, f32[6,5,32,8,128]{4,3,2,1,0:T(8,128)}, u32[]{:S(2)}) copy-start(f32[6,5,32,8,128]{4,3,2,1,0:T(8,128)} %copy-done) | copy-start | bytes 11796484
  36.8 44.9 %copy-start.4 = (f32[5]{0:T(128)S(1)}, f32[5]{0:T(128)}, u32[]{:S(2)}) copy-start(f32[5]{0:T(128)} %mob.1) | copy-start | bytes 64
  36.8 44.9 %copy-start.5 = (f32[5]{0:T(128)S(1)}, f32[5]{0:T(128)}, u32[]{:S(2)}) copy-start(f32[5]{0:T(128)} %gain.1) | copy-start | bytes 64
  36.8 44.9 %copy-start.6 = (f32[5]{0:T(128)S(1)}, f32[5]{0:T(128)}, u32[]{:S(2)}) copy-start(f32[5]{0:T(128)} %rates.1) | copy-start | bytes 64
  36.9 39.1 %collective-permute-start.4 = (f32[5,32,8,128]{3,2,1,0:T(8,128)S(1)}, f32[5,32,8,128]{3,2,1,0:T(8,128)S(1)}, u32[]{:S(2)}, u32[]{:S(2)}) collective-permute-start(f32[5,32,8,128]{3,2,1,0:T(8,128)S(1)} %get-tuple-element.29), channel_id=1, source_target_pairs={{0,1},{1,2},{2,3},{3,4},{4,5},{5,6},{6,7},{8,9},{9,10},{10,11},{11... | collective-permute-start | bytes 1966088 | tf_op jit(solution)/shard_map/ppermute | solution.py:390
  40.3 38.1 %collective-permute-start.5 = (f32[5,32,8,128]{3,2,1,0:T(8,128)S(1)}, f32[5,32,8,128]{3,2,1,0:T(8,128)S(1)}, u32[]{:S(2)}, u32[]{:S(2)}) collective-permute-start(f32[5,32,8,128]{3,2,1,0:T(8,128)S(1)} %get-tuple-element.30), channel_id=1, source_target_pairs={{1,0},{2,1},{3,2},{4,3},{5,4},{6,5},{7,6},{9,8},{10,9},{11,10},{12... | collective-permute-start | bytes 1966088 | tf_op jit(solution)/shard_map/ppermute | solution.py:390
  43.0 6.8 %collective-permute-start.8 = (f32[6,5,8,128]{3,2,1,0:T(8,128)S(1)}, f32[6,5,8,128]{3,2,1,0:T(8,128)S(1)}, u32[]{:S(2)}, u32[]{:S(2)}) collective-permute-start(f32[6,5,8,128]{3,2,1,0:T(8,128)S(1)} %get-tuple-element.37), channel_id=1, source_target_pairs={{0,16},{8,24},{1,17},{9,25},{2,18},{10,26},{3,19},{11,27},{4,20},{... | collective-permute-start | bytes 368648 | tf_op jit(solution)/shard_map/ppermute | solution.py:390
  49.8 35.4 %collective-permute-start.6 = (f32[12,5,8,128]{3,2,1,0:T(8,128)S(1)}, f32[12,5,8,128]{3,2,1,0:T(8,128)S(1)}, u32[]{:S(2)}, u32[]{:S(2)}) collective-permute-start(f32[12,5,8,128]{3,2,1,0:T(8,128)S(1)} %get-tuple-element.35), channel_id=1, source_target_pairs={{0,1},{1,2},{2,3},{3,4},{4,5},{5,6},{6,7},{8,9},{9,10},{10,11},{11... | collective-permute-start | bytes 737288 | tf_op jit(solution)/shard_map/ppermute | solution.py:390
  53.8 31.3 %collective-permute-start.7 = (f32[12,5,8,128]{3,2,1,0:T(8,128)S(1)}, f32[12,5,8,128]{3,2,1,0:T(8,128)S(1)}, u32[]{:S(2)}, u32[]{:S(2)}) collective-permute-start(f32[12,5,8,128]{3,2,1,0:T(8,128)S(1)} %get-tuple-element.36), channel_id=1, source_target_pairs={{1,0},{2,1},{3,2},{4,3},{5,4},{6,5},{7,6},{9,8},{10,9},{11,10},{12... | collective-permute-start | bytes 737288 | tf_op jit(solution)/shard_map/ppermute | solution.py:390
  55.8 27.4 %collective-permute-start.9 = (f32[6,5,8,128]{3,2,1,0:T(8,128)S(1)}, f32[6,5,8,128]{3,2,1,0:T(8,128)S(1)}, u32[]{:S(2)}, u32[]{:S(2)}) collective-permute-start(f32[6,5,8,128]{3,2,1,0:T(8,128)S(1)} %get-tuple-element.38), channel_id=1, source_target_pairs={{16,0},{24,8},{17,1},{25,9},{18,2},{26,10},{19,3},{27,11},{20,4},{... | collective-permute-start | bytes 368648 | tf_op jit(solution)/shard_map/ppermute | solution.py:390
  75.9 7.3 %collective-permute-start.10 = (f32[6,5,8,128]{3,2,1,0:T(8,128)S(1)}, f32[6,5,8,128]{3,2,1,0:T(8,128)S(1)}, u32[]{:S(2)}, u32[]{:S(2)}) collective-permute-start(f32[6,5,8,128]{3,2,1,0:T(8,128)S(1)} %get-tuple-element.39), channel_id=1, source_target_pairs={{0,2},{1,3},{2,4},{3,5},{4,6},{5,7},{8,10},{9,11},{10,12},{11,13},... | collective-permute-start | bytes 368648 | tf_op jit(solution)/shard_map/ppermute | solution.py:390
  78.4 6.8 %collective-permute-start.11 = (f32[6,5,8,128]{3,2,1,0:T(8,128)S(1)}, f32[6,5,8,128]{3,2,1,0:T(8,128)S(1)}, u32[]{:S(2)}, u32[]{:S(2)}) collective-permute-start(f32[6,5,8,128]{3,2,1,0:T(8,128)S(1)} %get-tuple-element.40), channel_id=1, source_target_pairs={{2,0},{3,1},{4,2},{5,3},{6,4},{7,5},{10,8},{11,9},{12,10},{13,11},... | collective-permute-start | bytes 368648 | tf_op jit(solution)/shard_map/ppermute | solution.py:390
where the time goes:
time: 93.1 us; the launch traced here: 92.7 us
  starting transfers between devices  35.3 us (38%)
  waiting for transfers between devices  27.2 us (29%)
  Pallas kernels  21.2 us (23%)
  local copies, waits for them, and re-layouts  7.8 us (8%)
    ppermute x12, starting transfers between devices, passed_along(): return lax.ppermute(x, axis, pairs)  29.2 us
    ppermute x12, waiting for transfers between devices, passed_along(): return lax.ppermute(x, axis, pairs)  22.2 us
    pallas_call x7, Pallas kernels, run(): pl.pallas_call(kernel, out_shape=out_shape, in_specs=in_specs, out_specs=...  21.2 us
    unnamed x18, local copies, waits for them, and re-layouts  6.51 us
    all_to_all x1, starting transfers between devices, gather(): return lax.all_to_all(sent, ('gx', 'gy'), 0, 0, tiled=True).reshape(-1)  6.07 us
    all_to_all x1, waiting for transfers between devices, gather(): return lax.all_to_all(sent, ('gx', 'gy'), 0, 0, tiled=True).reshape(-1)  5.03 us
  transfers between devices with their start and end apart: 13, of which 4 were waited for; matrix products, arithmetic and copies ran while one was open for 2% of the time, Pallas kernels for 10%

commit v1 on v0

--- a/solution.py
+++ b/solution.py
@@ -15,6 +15,7 @@
 MOVE = 1
 WORKING = KEEP - 1 + MOVE
 SIDES = 6
+SPARE = 4
 TILES = B * B // 128
 LAYER = (TILES, 128)
 PAD = 2 * TILES
@@ -23,8 +24,8 @@
 VMEM = pl.BlockSpec(memory_space=pltpu.VMEM)
 SMEM = pl.BlockSpec(memory_space=pltpu.SMEM)
 ANY = pl.BlockSpec(memory_space=pl.ANY)
+HBM = pl.BlockSpec(memory_space=pltpu.HBM)
 F32 = jnp.float32
-VMEM_LIMIT = 24 << 20
 
 
 def iotas():
@@ -53,10 +54,13 @@
         assert all((p * self.scale) >> 16 == p // cap for p in range(cap * devices))
 
     def gather(self, neighbours, source_slot):
-        own = jnp.concatenate([source_slot, neighbours.reshape(-1)])
-        own = jnp.pad(own, (0, self.width - own.shape[0]))
-        sent = jnp.broadcast_to(own[None], (self.devices, self.width))
-        return lax.all_to_all(sent, ("gx", "gy"), 0, 0, tiled=True).reshape(-1)
+        sent = call(
+            functools.partial(table_kernel, self),
+            shape(self.devices, 1, self.width, dtype=jnp.int32),
+            [SMEM, SMEM],
+            VMEM,
+        )(source_slot, neighbours)
+        return lax.all_to_all(sent, ("gx", "gy"), 0, 0, tiled=True)
 
     def device(self, slot):
         return (slot * self.scale) >> 16
@@ -65,7 +69,7 @@
         return jnp.clip(device, 0, self.devices - 1)
 
     def take(self, table, device, t):
-        return table[self.there(device) * self.width + t]
+        return table[self.there(device), 0, t]
 
     def local(self, slot, device):
         at = slot - device * self.cap
@@ -74,9 +78,20 @@
     def need(self, table, slot, side):
         safe = jnp.maximum(slot, 0)
         home = self.device(safe)
-        near = table[home * self.width + self.cap + (safe - home * self.cap) * SIDES + side]
+        near = table[home, 0, self.cap + (safe - home * self.cap) * SIDES + side]
         face = jnp.where(near < 0, side, side ^ 1)
         return jnp.where(slot < 0, -1, jnp.where(near < 0, slot, near)), face
+
+
+def table_kernel(info, source_slot, neighbours, out):
+    lane = lax.broadcasted_iota(jnp.int32, (1, info.width), 1)
+    row = jnp.zeros((1, info.width), jnp.int32)
+    for p in range(info.cap):
+        row = jnp.where(lane == p, source_slot[p], row)
+        for f in range(SIDES):
+            row = jnp.where(lane == info.cap + p * SIDES + f, neighbours[p, f], row)
+    for device in range(info.devices):
+        out[device] = row
 
 
 def each_side(body):
@@ -100,7 +115,7 @@
     return pick
 
 
-def pack_kernel(cap, c_ref, dense, faces, raw, sems):
+def pack_kernel(cap, c_ref, dense_ref, faces, raw, dense, sems, out_sems):
     for s in range(SPECIES):
         raw_copy(c_ref, raw, sems, cap, s).start()
     rows = raw_rows(raw)
@@ -108,11 +123,16 @@
     z = lane & (B - 1)
     quarter = lane // B
 
+    def copy_out(s):
+        return pltpu.make_async_copy(
+            dense.at[:, s], dense_ref.at[pl.ds(0, cap), s], out_sems.at[s]
+        )
+
     def species(s, carry):
         raw_copy(c_ref, raw, sems, cap, s).wait()
         base = s * PER_S
 
-        def slot(p, carry2):
+        for p in range(cap):
             start = base + p
             z_first = z_last = None
             for x in range(B):
@@ -138,42 +158,48 @@
             faces[p * SIDES + 3, s] = y_last
             faces[p * SIDES + 4, s] = z_first
             faces[p * SIDES + 5, s] = z_last
-            return carry2
-
-        return lax.fori_loop(0, cap, slot, carry)
+        copy_out(s).start()
+        return carry
 
     lax.fori_loop(0, SPECIES, species, 0)
-
-
-def copy_patches(pairs, dense):
-    def layer(x, carry):
-        for s in range(SPECIES):
-            for number, out in pairs:
-                out[s, x] = dense[number, s, x]
-        return carry
-
-    lax.fori_loop(0, B, layer, 0, unroll=4)
-
-
-def first_kernel(info, me_ref, table, dense, to_yp, to_ym):
+    for s in range(SPECIES):
+        copy_out(s).wait()
+
+
+def patch_copies(pairs, dense, sems):
+    return [
+        pltpu.make_async_copy(dense.at[number], out, sems.at[i])
+        for i, (number, out) in enumerate(pairs)
+    ]
+
+
+def first_kernel(info, me_ref, table, dense, to_yp, to_ym, sems):
     me = me_ref[0]
     up, down = picked(info, table, me, me + 1), picked(info, table, me, me - 1)
-    copy_patches(((up, to_yp), (down, to_ym)), dense)
+    copies = patch_copies(((up, to_yp), (down, to_ym)), dense, sems)
+    for copy in copies:
+        copy.start()
+    for copy in copies:
+        copy.wait()
 
 
 def second_kernel(
-    info, me_ref, table, dense, faces, to_xp, to_xm, to_x2p, to_x2m, to_y2p, to_y2m, patches
+    info, me_ref, table, dense, faces, to_xp, to_xm, to_x2p, to_x2m, to_y2p, to_y2m, own, patches,
+    sems,
 ):
     me = me_ref[0]
     up, down = picked(info, table, me, me + info.rows), picked(info, table, me, me - info.rows)
-    copy_patches(((up, to_xp), (down, to_xm)), dense)
+    kept = [info.local(info.take(table, me, t), me)[1] for t in range(WORKING)]
+    pairs = [(up, to_xp), (down, to_xm), *((kept[t], own.at[t]) for t in range(WORKING))]
+    copies = patch_copies(pairs, dense, sems)
+    for copy in copies:
+        copy.start()
     for t in range(WORKING):
         slot = info.take(table, me, t)
         kind = jnp.int32(-1)
         for c, device in enumerate((me, me - info.rows, me + info.rows, me - 1, me + 1)):
             kind = jnp.where((slot >= 0) & info.local(slot, device)[0], c, kind)
         patches[t] = kind
-        patches[WORKING + t] = info.local(slot, me)[1]
 
     for step, out in ((info.rows, to_x2p), (-info.rows, to_x2m), (1, to_y2p), (-1, to_y2m)):
         for t in range(WORKING):
@@ -189,6 +215,9 @@
                     pl.when(here)(
                         functools.partial(copy_face, out, f, faces, at * SIDES + face)
                     )
+
+    for copy in copies:
+        copy.wait()
 
 
 def faces_kernel(info, me_ref, table, f_own, f_xm, f_xp, to_yp, to_ym, ghosts, plan):
@@ -225,7 +254,7 @@
 
 
 def prepare_kernel(
-    patches, mob, gain, rates, dense, p_xm, p_xp, p_ym, p_yp, grid, fixed, factor
+    patches, mob, gain, rates, own, p_xm, p_xp, p_ym, p_yp, grid, fixed, factor
 ):
     zero = jnp.zeros(LAYER, F32)
 
@@ -266,7 +295,7 @@
 
         kind = patches[t]
         pl.when(kind == 0)(
-            functools.partial(prepare, lambda s, x, t=t: dense[patches[WORKING + t], s, x])
+            functools.partial(prepare, lambda s, x, t=t: own[t, s, x])
         )
         for c, src in ((1, p_xm), (2, p_xp), (3, p_ym), (4, p_yp)):
             pl.when(kind == c)(functools.partial(prepare, lambda s, x, src=src: src[s, x]))
@@ -394,7 +423,7 @@
     return passed_along(up, axis, by), passed_along(down, axis, -by)
 
 
-def call(kernel, out_shape, in_specs, out_specs, scratch=(), aliases=None):
+def call(kernel, out_shape, in_specs, out_specs, scratch=(), aliases=None, mib=2):
     def run(*args):
         return pl.pallas_call(
             kernel,
@@ -403,7 +432,7 @@
             out_specs=out_specs,
             scratch_shapes=list(scratch),
             input_output_aliases=aliases or {},
-            compiler_params=pltpu.CompilerParams(vmem_limit_bytes=VMEM_LIMIT),
+            compiler_params=pltpu.CompilerParams(vmem_limit_bytes=mib << 20),
         )(*args)
 
     return run
@@ -426,14 +455,19 @@
     two_patches = shape(WORKING, species, B, *LAYER)
     all_sides = shape(WORKING * SIDES, species, *LAYER)
     one_patch = shape(SIDES, species, *LAYER)
-    pack = call(
+    dense, faces = call(
         functools.partial(pack_kernel, cap),
-        (shape(cap, species, B, *LAYER), shape(cap * SIDES, species, *LAYER)),
-        [ANY],
-        (VMEM, VMEM),
-        [pltpu.VMEM((species, tiles, 8, 128), F32), pltpu.SemaphoreType.DMA((species,))],
-    )
-    dense, faces = pack(view)
+        (shape(SPARE * cap, species, B, *LAYER), shape(cap * SIDES, species, *LAYER)),
+        [HBM],
+        (HBM, VMEM),
+        [
+            pltpu.VMEM((species, tiles, 8, 128), F32),
+            pltpu.VMEM((cap, species, B, *LAYER), F32),
+            pltpu.SemaphoreType.DMA((species,)),
+            pltpu.SemaphoreType.DMA((species,)),
+        ],
+        mib=57,
+    )(view)
     blank = call(
         functools.partial(blank_kernel, cap),
         shape(species, tiles, cap, 128),
@@ -443,16 +477,20 @@
     )()
 
     s_yp, s_ym = call(
-        functools.partial(first_kernel, info), (patch,) * 2, [SMEM, SMEM, VMEM], (VMEM,) * 2
+        functools.partial(first_kernel, info), (patch,) * 2, [SMEM, SMEM, HBM], (VMEM,) * 2,
+        [pltpu.SemaphoreType.DMA((2,))],
+        mib=50,
     )(me, table, dense)
     p_ym, p_yp = both_ways(s_yp, s_ym, "gy", 1)
     f_xm, f_xp = both_ways(faces, faces, "gx", 1)
 
-    s_xp, s_xm, t_x2p, t_x2m, t_y2p, t_y2m, patches = call(
+    s_xp, s_xm, t_x2p, t_x2m, t_y2p, t_y2m, own, patches = call(
         functools.partial(second_kernel, info),
-        (patch, patch) + (one_patch,) * 4 + (shape(2 * WORKING, dtype=jnp.int32),),
-        [SMEM, SMEM, VMEM, VMEM],
-        (VMEM,) * 6 + (SMEM,),
+        (patch, patch) + (one_patch,) * 4 + (two_patches, shape(WORKING, dtype=jnp.int32)),
+        [SMEM, SMEM, HBM, VMEM],
+        (VMEM,) * 7 + (SMEM,),
+        [pltpu.SemaphoreType.DMA((2 + WORKING,))],
+        mib=50,
     )(me, table, dense, faces)
     p_xm, p_xp = both_ways(s_xp, s_xm, "gx", 1)
 
@@ -469,7 +507,7 @@
     padded = shape(WORKING, species, B * PAD + TILES, 128)
     grid, fixed, factor = call(
         prepare_kernel, (padded, two_patches, two_patches), [SMEM] * 4 + [VMEM] * 5, (VMEM,) * 3
-    )(patches, mobility, fermi_gain, rates, dense, p_xm, p_xp, p_ym, p_yp)
+    )(patches, mobility, fermi_gain, rates, own, p_xm, p_xp, p_ym, p_yp)
 
     moved = call(
         sweep_kernel,
@@ -484,6 +522,7 @@
             pltpu.SemaphoreType.DMA((species,)),
         ],
         {12: 0},
+        mib=10,
     )(patches, plan, grid, fixed, factor, ghosts, g_ym, g_yp, g_x2m, g_x2p, g_y2m, g_y2p, blank)
     return moved.transpose(2, 0, 1, 3).reshape(cap, species, cells)
 

time: 93.1 us -> 93.4 us (level); the launches traced: 92.7 us -> 91.6 us
  local copies, waits for them, and re-layouts: 7.8 us -> 1.15 us
  Pallas kernels: 21.2 us -> 26.4 us
  starting transfers between devices: 35.3 us -> 38.9 us
  waiting for transfers between devices: 27.2 us -> 24.8 us
    unnamed x18 -> x14, local copies, waits for them, and re-layouts: 6.51 us -> 1.15 us
    pallas_call x7 -> x8, Pallas kernels: 21.2 us -> 26.4 us  [run(): pl.pallas_call(kernel, out_shape=out_shape, in_specs=in_specs, out_specs=...]
    ppermute x12, starting transfers between devices: 29.2 us -> 32.8 us  [passed_along(): return lax.ppermute(x, axis, pairs)]
    ppermute x12, waiting for transfers between devices: 22.2 us -> 19.7 us  [passed_along(): return lax.ppermute(x, axis, pairs)]
  transfers between devices with their start and end apart: 13 -> 13, of which waited for: 4 -> 3; matrix products, arithmetic and copies ran while one was open for 2% -> 0% of each run, Pallas kernels for 10% -> 15%
where the time goes in v1:
time: 93.4 us; the launch traced here: 91.6 us
  starting transfers between devices  38.9 us (42%)
  Pallas kernels  26.4 us (28%)
  waiting for transfers between devices  24.8 us (27%)
  local copies, waits for them, and re-layouts  1.15 us (1%)
    ppermute x12, starting transfers between devices, passed_along(): return lax.ppermute(x, axis, pairs)  32.8 us
    pallas_call x8, Pallas kernels, run(): pl.pallas_call(kernel, out_shape=out_shape, in_specs=in_specs, out_specs=...  26.4 us
    ppermute x12, waiting for transfers between devices, passed_along(): return lax.ppermute(x, axis, pairs)  19.7 us
    all_to_all x1, starting transfers between devices, gather(): return lax.all_to_all(sent, ('gx', 'gy'), 0, 0, tiled=True)  6.07 us
    all_to_all x1, waiting for transfers between devices, gather(): return lax.all_to_all(sent, ('gx', 'gy'), 0, 0, tiled=True)  5.11 us
  transfers between devices with their start and end apart: 13, of which 3 were waited for; matrix products, arithmetic and copies ran while one was open for 0% of the time, Pallas kernels for 15%

profile of v1, /device:TPU:6, one launch (start us, length us, event | category | flops | bytes accessed | tf_op | source)
XLA Modules:
  0.0 91.6 jit_solution(546310255311444874)
XLA Ops:
  0.0 0.0 copy-start.2
  0.0 0.0 copy-start.6
  0.0 5.5 %shard_map.65 = (f32[24,5,32,8,128]{4,3,2,1,0:T(8,128)}, f32[36,5,8,128]{3,2,1,0:T(8,128)}) custom-call(f32[5,256,6,128]{3,2,1,0:T(8,128)} %bitcast.7), custom_call_target="tpu_custom_call" | custom-call | tf_op jit(solution)/shard_map/pallas_call | solution.py:428
  5.5 1.9 %collective-permute-start = (f32[36,5,8,128]{3,2,1,0:T(8,128)}, f32[36,5,8,128]{3,2,1,0:T(8,128)S(1)}, u32[]{:S(2)}, u32[]{:S(2)}) collective-permute-start(f32[36,5,8,128]{3,2,1,0:T(8,128)} %get-tuple-element.25.faces.f_own), channel_id=1, source_target_pairs={{0,8},{8,16},{16,24},{1,9},{9,17},{17,25},{2,10},{10,18},{18,26},{... | collective-permute-start | bytes 2211848 | tf_op jit(solution)/shard_map/ppermute | solution.py:419
  7.5 3.6 %collective-permute-start.1 = (f32[36,5,8,128]{3,2,1,0:T(8,128)}, f32[36,5,8,128]{3,2,1,0:T(8,128)S(1)}, u32[]{:S(2)}, u32[]{:S(2)}) collective-permute-start(f32[36,5,8,128]{3,2,1,0:T(8,128)} %get-tuple-element.25.faces.f_own), channel_id=1, source_target_pairs={{8,0},{16,8},{24,16},{9,1},{17,9},{25,17},{10,2},{18,10},{26,18},{... | collective-permute-start | bytes 2211848 | tf_op jit(solution)/shard_map/ppermute | solution.py:419
  11.1 0.0 copy-done.2
  11.1 0.0 copy-done.6
  11.1 1.2 %shard_map.64 = s32[32,1,48]{2,1,0:T(1,128)} custom-call(s32[6]{0:T(128)S(1)} %copy-done.6, s32[6,6]{1,0:T(8,128)S(1)} %copy-done.2), custom_call_target="tpu_custom_call" | custom-call | tf_op jit(solution)/shard_map/pallas_call | solution.py:428
  12.4 6.1 %all-to-all-start = ((s32[32,1,48]{2,1,0:T(1,128)}), s32[32,1,48]{2,1,0:T(1,128)S(1)}, u32[]{:S(2)}, u32[]{:S(2)}) async-start(s32[32,1,48]{2,1,0:T(1,128)} %shard_map.64), calls=%async_computation | async-start | bytes 32768 | tf_op jit(solution)/shard_map/all_to_all | solution.py:63
  18.5 5.1 %all-to-all-done.table = s32[32,1,48]{2,1,0:T(1,128)S(1)} async-done(((s32[32,1,48]{2,1,0:T(1,128)}), s32[32,1,48]{2,1,0:T(1,128)S(1)}, u32[]{:S(2)}, u32[]{:S(2)}) %all-to-all-start) | async-done | bytes 6176 | tf_op jit(solution)/shard_map/all_to_all | solution.py:63
  23.6 0.0 copy-start
  23.6 1.1 %copy-done = f32[36,5,8,128]{3,2,1,0:T(8,128)S(1)} copy-done((f32[36,5,8,128]{3,2,1,0:T(8,128)S(1)}, f32[36,5,8,128]{3,2,1,0:T(8,128)}, u32[]{:S(2)}) %copy-start) | copy-done | bytes 737304
  24.7 3.1 %shard_map.66 = (f32[5,32,8,128]{3,2,1,0:T(8,128)S(1)}, f32[5,32,8,128]{3,2,1,0:T(8,128)S(1)}, f32[6,5,8,128]{3,2,1,0:T(8,128)S(1)}, f32[6,5,8,128]{3,2,1,0:T(8,...) custom-call(s32[1]{0:T(128)} %bitcast.me_ref, ...), custom_call_target="tpu_custom_call" | custom-call | tf_op jit(solution)/shard_map/pallas_call | solution.py:428
  27.8 1.9 %collective-permute-start.2 = (f32[5,32,8,128]{3,2,1,0:T(8,128)S(1)}, f32[5,32,8,128]{3,2,1,0:T(8,128)S(1)}, u32[]{:S(2)}, u32[]{:S(2)}) collective-permute-start(f32[5,32,8,128]{3,2,1,0:T(8,128)S(1)} %get-tuple-element.29), channel_id=1, source_target_pairs={{0,8},{8,16},{16,24},{1,9},{9,17},{17,25},{2,10},{10,18},{18,26},{... | collective-permute-start | bytes 1966088 | tf_op jit(solution)/shard_map/ppermute | solution.py:419
  29.7 0.0 copy-start.1
  29.8 3.8 %collective-permute-start.3 = (f32[5,32,8,128]{3,2,1,0:T(8,128)S(1)}, f32[5,32,8,128]{3,2,1,0:T(8,128)S(1)}, u32[]{:S(2)}, u32[]{:S(2)}) collective-permute-start(f32[5,32,8,128]{3,2,1,0:T(8,128)S(1)} %get-tuple-element.30), channel_id=1, source_target_pairs={{8,0},{16,8},{24,16},{9,1},{17,9},{25,17},{10,2},{18,10},{26,18},{... | collective-permute-start | bytes 1966088 | tf_op jit(solution)/shard_map/ppermute | solution.py:419
  33.5 2.2 %shard_map.68 = (f32[5,32,8,128]{3,2,1,0:T(8,128)S(1)}, f32[5,32,8,128]{3,2,1,0:T(8,128)S(1)}) custom-call(s32[1]{0:T(128)} %bitcast.me_ref, s32[32,1,48]{2,1,0:T(1,128)S(1)} %all-to-all-done.table, f32[24,5,32,8,128]{4,3,2,1,0:T(8,128)} %get-tuple-element.24.dense), custom_call_target="tpu_custom_call" | custom-call | tf_op jit(solution)/shard_map/pallas_call | solution.py:428
  35.7 0.0 copy-start.3
  35.7 0.0 copy-start.4
  35.7 0.0 copy-start.5
  35.7 3.4 %collective-permute-start.4 = (f32[5,32,8,128]{3,2,1,0:T(8,128)S(1)}, f32[5,32,8,128]{3,2,1,0:T(8,128)S(1)}, u32[]{:S(2)}, u32[]{:S(2)}) collective-permute-start(f32[5,32,8,128]{3,2,1,0:T(8,128)S(1)} %get-tuple-element.31), channel_id=1, source_target_pairs={{0,1},{1,2},{2,3},{3,4},{4,5},{5,6},{6,7},{8,9},{9,10},{10,11},{11... | collective-permute-start | bytes 1966088 | tf_op jit(solution)/shard_map/ppermute | solution.py:419
  39.1 0.0 collective-permute-done.f_xm
  39.1 2.6 %collective-permute-start.5 = (f32[5,32,8,128]{3,2,1,0:T(8,128)S(1)}, f32[5,32,8,128]{3,2,1,0:T(8,128)S(1)}, u32[]{:S(2)}, u32[]{:S(2)}) collective-permute-start(f32[5,32,8,128]{3,2,1,0:T(8,128)S(1)} %get-tuple-element.32), channel_id=1, source_target_pairs={{1,0},{2,1},{3,2},{4,3},{5,4},{6,5},{7,6},{9,8},{10,9},{11,10},{12... | collective-permute-start | bytes 1966088 | tf_op jit(solution)/shard_map/ppermute | solution.py:419
  41.8 0.0 collective-permute-done.1.f_xp
  41.8 2.6 %collective-permute-start.10 = (f32[6,5,8,128]{3,2,1,0:T(8,128)S(1)}, f32[6,5,8,128]{3,2,1,0:T(8,128)S(1)}, u32[]{:S(2)}, u32[]{:S(2)}) collective-permute-start(f32[6,5,8,128]{3,2,1,0:T(8,128)S(1)} %get-tuple-element.41), channel_id=1, source_target_pairs={{0,2},{1,3},{2,4},{3,5},{4,6},{5,7},{8,10},{9,11},{10,12},{11,13},... | collective-permute-start | bytes 368648 | tf_op jit(solution)/shard_map/ppermute | solution.py:419
  44.4 0.0 copy-done.1
  44.4 3.4 %shard_map.67 = (f32[12,5,8,128]{3,2,1,0:T(8,128)S(1)}, f32[12,5,8,128]{3,2,1,0:T(8,128)S(1)}, f32[12,5,8,128]{3,2,1,0:T(8,128)S(1)}, s32[24]{0:T(128)S(1)}) custom-call(s32[1]{0:T(128)} %bitcast.me_ref, s32[32,1,48]{2,1,0:T(1,128)S(1)} %all-to-all-done.table, f32[36,5,8,128]{3,2,1,0:T(8,128)S(1)} %copy-done.1, ...), custom_call_target="tpu_custom_call" | custom-call | tf_op jit(solution)/shard_map/pallas_call | solution.py:428
  47.8 7.1 %collective-permute-done.10.g_y2m = f32[6,5,8,128]{3,2,1,0:T(8,128)S(1)} collective-permute-done((f32[6,5,8,128]{3,2,1,0:T(8,128)S(1)}, f32[6,5,8,128]{3,2,1,0:T(8,128)S(1)}, u32[]{:S(2)}, u32[]{:S(2)}) %collective-permute-start.10) | collective-permute-done | bytes 122912 | tf_op jit(solution)/shard_map/ppermute | solution.py:419
  54.9 1.9 %collective-permute-start.6 = (f32[12,5,8,128]{3,2,1,0:T(8,128)S(1)}, f32[12,5,8,128]{3,2,1,0:T(8,128)S(1)}, u32[]{:S(2)}, u32[]{:S(2)}) collective-permute-start(f32[12,5,8,128]{3,2,1,0:T(8,128)S(1)} %get-tuple-element.37), channel_id=1, source_target_pairs={{0,1},{1,2},{2,3},{3,4},{4,5},{5,6},{6,7},{8,9},{9,10},{10,11},{11... | collective-permute-start | bytes 737288 | tf_op jit(solution)/shard_map/ppermute | solution.py:419
  56.8 0.0 collective-permute-done.2.p_xm
  56.8 3.9 %collective-permute-start.7 = (f32[12,5,8,128]{3,2,1,0:T(8,128)S(1)}, f32[12,5,8,128]{3,2,1,0:T(8,128)S(1)}, u32[]{:S(2)}, u32[]{:S(2)}) collective-permute-start(f32[12,5,8,128]{3,2,1,0:T(8,128)S(1)} %get-tuple-element.38), channel_id=1, source_target_pairs={{1,0},{2,1},{3,2},{4,3},{5,4},{6,5},{7,6},{9,8},{10,9},{11,10},{12... | collective-permute-start | bytes 737288 | tf_op jit(solution)/shard_map/ppermute | solution.py:419
  60.7 0.0 collective-permute-done.3.p_xp
  60.7 1.3 %collective-permute-start.11 = (f32[6,5,8,128]{3,2,1,0:T(8,128)S(1)}, f32[6,5,8,128]{3,2,1,0:T(8,128)S(1)}, u32[]{:S(2)}, u32[]{:S(2)}) collective-permute-start(f32[6,5,8,128]{3,2,1,0:T(8,128)S(1)} %get-tuple-element.42), channel_id=1, source_target_pairs={{2,0},{3,1},{4,2},{5,3},{6,4},{7,5},{10,8},{11,9},{12,10},{13,11},... | collective-permute-start | bytes 368648 | tf_op jit(solution)/shard_map/ppermute | solution.py:419
  62.0 12.6 %collective-permute-done.4.p_ym = f32[5,32,8,128]{3,2,1,0:T(8,128)S(1)} collective-permute-done((f32[5,32,8,128]{3,2,1,0:T(8,128)S(1)}, f32[5,32,8,128]{3,2,1,0:T(8,128)S(1)}, u32[]{:S(2)}, u32[]{:S(2)}) %collective-permute-start.4) | collective-permute-done | bytes 655392 | tf_op jit(solution)/shard_map/ppermute | solution.py:419
  74.7 1.3 %collective-permute-start.8 = (f32[6,5,8,128]{3,2,1,0:T(8,128)S(1)}, f32[6,5,8,128]{3,2,1,0:T(8,128)S(1)}, u32[]{:S(2)}, u32[]{:S(2)}) collective-permute-start(f32[6,5,8,128]{3,2,1,0:T(8,128)S(1)} %get-tuple-element.39), channel_id=1, source_target_pairs={{0,16},{8,24},{1,17},{9,25},{2,18},{10,26},{3,19},{11,27},{4,20},{... | collective-permute-start | bytes 368648 | tf_op jit(solution)/shard_map/ppermute | solution.py:419
  76.0 0.0 collective-permute-done.5.p_yp
  76.0 4.6 %collective-permute-start.9 = (f32[6,5,8,128]{3,2,1,0:T(8,128)S(1)}, f32[6,5,8,128]{3,2,1,0:T(8,128)S(1)}, u32[]{:S(2)}, u32[]{:S(2)}) collective-permute-start(f32[6,5,8,128]{3,2,1,0:T(8,128)S(1)} %get-tuple-element.40), channel_id=1, source_target_pairs={{16,0},{24,8},{17,1},{25,9},{18,2},{26,10},{19,3},{27,11},{20,4},{... | collective-permute-start | bytes 368648 | tf_op jit(solution)/shard_map/ppermute | solution.py:419
  80.5 2.0 %shard_map.70.blank = f32[5,256,6,128]{3,2,1,0:T(8,128)} custom-call(), custom_call_target="tpu_custom_call" | custom-call | tf_op jit(solution)/shard_map/pallas_call | solution.py:428
  82.6 0.0 copy-done.3
  82.6 0.0 copy-done.4
  82.6 0.0 copy-done.5
  82.6 1.4 %shard_map.69 = (f32[2,5,520,128]{3,2,1,0:T(8,128)S(1)}, f32[2,5,32,8,128]{4,3,2,1,0:T(8,128)S(1)}, f32[2,5,32,8,128]{4,3,2,1,0:T(8,128)S(1)}) custom-call(s32[2]{0:T(128)S(1)} %get-tuple-element.26.patches, f32[5]{0:T(128)S(1)} %copy-done.3, f32[5]{0:T(128)S(1)} %copy-done.4, f32[5]{0:T(128)S(1)} %copy-done.5, ...), custom_call_target="tpu_custom_call" | custom-call | tf_op jit(solution)/shard_map/pallas_call | solution.py:428
  84.0 0.0 collective-permute-done.11.g_y2p
  84.0 0.0 collective-permute-done.8.g_xm
  84.0 0.0 collective-permute-done.9.g_xp
  84.1 0.0 collective-permute-done.6.g_ym
  84.1 0.0 collective-permute-done.7.g_yp
  84.1 7.5 %shard_map.71 = f32[5,256,6,128]{3,2,1,0:T(8,128)} custom-call(s32[2]{0:T(128)S(1)} %get-tuple-element.26.patches, s32[24]{0:T(128)S(1)} %get-tuple-element.27.plan, f32[2,5,520,128]{3,2,1,0:T(8,128)S(1)} %get-tuple-element.33.grid, f32[2,5,32,8,128]{4,3,2,1,0:T(8,128)S(1)} %get-tuple-element.34.fixed, ...), custom_call_target="tpu_custom_call", output_to_operand_aliasing={{}: (12, {})} | custom-call | tf_op jit(solution)/shard_map/pallas_call | solution.py:428
Async XLA Ops:
  0.0 11.1 %copy-start.2 = (s32[6,6]{1,0:T(8,128)S(1)}, s32[6,6]{1,0:T(8,128)}, u32[]{:S(2)}) copy-start(s32[6,6]{1,0:T(8,128)} %neighbours.1) | copy-start | bytes 436
  0.0 11.1 %copy-start.6 = (s32[6]{0:T(128)S(1)}, s32[6]{0:T(128)}, u32[]{:S(2)}) copy-start(s32[6]{0:T(128)} %source_slot.1) | copy-start | bytes 76
  5.5 33.6 %collective-permute-start = (f32[36,5,8,128]{3,2,1,0:T(8,128)}, f32[36,5,8,128]{3,2,1,0:T(8,128)S(1)}, u32[]{:S(2)}, u32[]{:S(2)}) collective-permute-start(f32[36,5,8,128]{3,2,1,0:T(8,128)} %get-tuple-element.25.faces.f_own), channel_id=1, source_target_pairs={{0,8},{8,16},{16,24},{1,9},{9,17},{17,25},{2,10},{10,18},{18,26},{... | collective-permute-start | bytes 2211848 | tf_op jit(solution)/shard_map/ppermute | solution.py:419
  7.5 34.3 %collective-permute-start.1 = (f32[36,5,8,128]{3,2,1,0:T(8,128)}, f32[36,5,8,128]{3,2,1,0:T(8,128)S(1)}, u32[]{:S(2)}, u32[]{:S(2)}) collective-permute-start(f32[36,5,8,128]{3,2,1,0:T(8,128)} %get-tuple-element.25.faces.f_own), channel_id=1, source_target_pairs={{8,0},{16,8},{24,16},{9,1},{17,9},{25,17},{10,2},{18,10},{26,18},{... | collective-permute-start | bytes 2211848 | tf_op jit(solution)/shard_map/ppermute | solution.py:419
  12.4 11.2 %all-to-all-start = ((s32[32,1,48]{2,1,0:T(1,128)}), s32[32,1,48]{2,1,0:T(1,128)S(1)}, u32[]{:S(2)}, u32[]{:S(2)}) async-start(s32[32,1,48]{2,1,0:T(1,128)} %shard_map.64), calls=%async_computation | async-start | bytes 32768 | tf_op jit(solution)/shard_map/all_to_all | solution.py:63
  23.6 1.1 %copy-start = (f32[36,5,8,128]{3,2,1,0:T(8,128)S(1)}, f32[36,5,8,128]{3,2,1,0:T(8,128)}, u32[]{:S(2)}) copy-start(f32[36,5,8,128]{3,2,1,0:T(8,128)} %get-tuple-element.25.faces.f_own) | copy-start | bytes 2211844
  27.8 29.0 %collective-permute-start.2 = (f32[5,32,8,128]{3,2,1,0:T(8,128)S(1)}, f32[5,32,8,128]{3,2,1,0:T(8,128)S(1)}, u32[]{:S(2)}, u32[]{:S(2)}) collective-permute-start(f32[5,32,8,128]{3,2,1,0:T(8,128)S(1)} %get-tuple-element.29), channel_id=1, source_target_pairs={{0,8},{8,16},{16,24},{1,9},{9,17},{17,25},{2,10},{10,18},{18,26},{... | collective-permute-start | bytes 1966088 | tf_op jit(solution)/shard_map/ppermute | solution.py:419
  29.7 14.7 %copy-start.1 = (f32[36,5,8,128]{3,2,1,0:T(8,128)S(1)}, f32[36,5,8,128]{3,2,1,0:T(8,128)}, u32[]{:S(2)}) copy-start(f32[36,5,8,128]{3,2,1,0:T(8,128)} %get-tuple-element.25.faces.f_own) | copy-start | bytes 2211844
  29.8 31.0 %collective-permute-start.3 = (f32[5,32,8,128]{3,2,1,0:T(8,128)S(1)}, f32[5,32,8,128]{3,2,1,0:T(8,128)S(1)}, u32[]{:S(2)}, u32[]{:S(2)}) collective-permute-start(f32[5,32,8,128]{3,2,1,0:T(8,128)S(1)} %get-tuple-element.30), channel_id=1, source_target_pairs={{8,0},{16,8},{24,16},{9,1},{17,9},{25,17},{10,2},{18,10},{26,18},{... | collective-permute-start | bytes 1966088 | tf_op jit(solution)/shard_map/ppermute | solution.py:419
  35.7 46.9 %copy-start.3 = (f32[5]{0:T(128)S(1)}, f32[5]{0:T(128)}, u32[]{:S(2)}) copy-start(f32[5]{0:T(128)} %mob.1) | copy-start | bytes 64
  35.7 46.9 %copy-start.4 = (f32[5]{0:T(128)S(1)}, f32[5]{0:T(128)}, u32[]{:S(2)}) copy-start(f32[5]{0:T(128)} %gain.1) | copy-start | bytes 64
  35.7 46.9 %copy-start.5 = (f32[5]{0:T(128)S(1)}, f32[5]{0:T(128)}, u32[]{:S(2)}) copy-start(f32[5]{0:T(128)} %rates.1) | copy-start | bytes 64
  35.7 38.9 %collective-permute-start.4 = (f32[5,32,8,128]{3,2,1,0:T(8,128)S(1)}, f32[5,32,8,128]{3,2,1,0:T(8,128)S(1)}, u32[]{:S(2)}, u32[]{:S(2)}) collective-permute-start(f32[5,32,8,128]{3,2,1,0:T(8,128)S(1)} %get-tuple-element.31), channel_id=1, source_target_pairs={{0,1},{1,2},{2,3},{3,4},{4,5},{5,6},{6,7},{8,9},{9,10},{10,11},{11... | collective-permute-start | bytes 1966088 | tf_op jit(solution)/shard_map/ppermute | solution.py:419
  39.1 36.8 %collective-permute-start.5 = (f32[5,32,8,128]{3,2,1,0:T(8,128)S(1)}, f32[5,32,8,128]{3,2,1,0:T(8,128)S(1)}, u32[]{:S(2)}, u32[]{:S(2)}) collective-permute-start(f32[5,32,8,128]{3,2,1,0:T(8,128)S(1)} %get-tuple-element.32), channel_id=1, source_target_pairs={{1,0},{2,1},{3,2},{4,3},{5,4},{6,5},{7,6},{9,8},{10,9},{11,10},{12... | collective-permute-start | bytes 1966088 | tf_op jit(solution)/shard_map/ppermute | solution.py:419
  41.8 13.1 %collective-permute-start.10 = (f32[6,5,8,128]{3,2,1,0:T(8,128)S(1)}, f32[6,5,8,128]{3,2,1,0:T(8,128)S(1)}, u32[]{:S(2)}, u32[]{:S(2)}) collective-permute-start(f32[6,5,8,128]{3,2,1,0:T(8,128)S(1)} %get-tuple-element.41), channel_id=1, source_target_pairs={{0,2},{1,3},{2,4},{3,5},{4,6},{5,7},{8,10},{9,11},{10,12},{11,13},... | collective-permute-start | bytes 368648 | tf_op jit(solution)/shard_map/ppermute | solution.py:419
  54.9 29.2 %collective-permute-start.6 = (f32[12,5,8,128]{3,2,1,0:T(8,128)S(1)}, f32[12,5,8,128]{3,2,1,0:T(8,128)S(1)}, u32[]{:S(2)}, u32[]{:S(2)}) collective-permute-start(f32[12,5,8,128]{3,2,1,0:T(8,128)S(1)} %get-tuple-element.37), channel_id=1, source_target_pairs={{0,1},{1,2},{2,3},{3,4},{4,5},{5,6},{6,7},{8,9},{9,10},{10,11},{11... | collective-permute-start | bytes 737288 | tf_op jit(solution)/shard_map/ppermute | solution.py:419
  56.8 27.3 %collective-permute-start.7 = (f32[12,5,8,128]{3,2,1,0:T(8,128)S(1)}, f32[12,5,8,128]{3,2,1,0:T(8,128)S(1)}, u32[]{:S(2)}, u32[]{:S(2)}) collective-permute-start(f32[12,5,8,128]{3,2,1,0:T(8,128)S(1)} %get-tuple-element.38), channel_id=1, source_target_pairs={{1,0},{2,1},{3,2},{4,3},{5,4},{6,5},{7,6},{9,8},{10,9},{11,10},{12... | collective-permute-start | bytes 737288 | tf_op jit(solution)/shard_map/ppermute | solution.py:419
  60.7 23.3 %collective-permute-start.11 = (f32[6,5,8,128]{3,2,1,0:T(8,128)S(1)}, f32[6,5,8,128]{3,2,1,0:T(8,128)S(1)}, u32[]{:S(2)}, u32[]{:S(2)}) collective-permute-start(f32[6,5,8,128]{3,2,1,0:T(8,128)S(1)} %get-tuple-element.42), channel_id=1, source_target_pairs={{2,0},{3,1},{4,2},{5,3},{6,4},{7,5},{10,8},{11,9},{12,10},{13,11},... | collective-permute-start | bytes 368648 | tf_op jit(solution)/shard_map/ppermute | solution.py:419
  74.7 9.3 %collective-permute-start.8 = (f32[6,5,8,128]{3,2,1,0:T(8,128)S(1)}, f32[6,5,8,128]{3,2,1,0:T(8,128)S(1)}, u32[]{:S(2)}, u32[]{:S(2)}) collective-permute-start(f32[6,5,8,128]{3,2,1,0:T(8,128)S(1)} %get-tuple-element.39), channel_id=1, source_target_pairs={{0,16},{8,24},{1,17},{9,25},{2,18},{10,26},{3,19},{11,27},{4,20},{... | collective-permute-start | bytes 368648 | tf_op jit(solution)/shard_map/ppermute | solution.py:419
  76.0 8.1 %collective-permute-start.9 = (f32[6,5,8,128]{3,2,1,0:T(8,128)S(1)}, f32[6,5,8,128]{3,2,1,0:T(8,128)S(1)}, u32[]{:S(2)}, u32[]{:S(2)}) collective-permute-start(f32[6,5,8,128]{3,2,1,0:T(8,128)S(1)} %get-tuple-element.40), channel_id=1, source_target_pairs={{16,0},{24,8},{17,1},{25,9},{18,2},{26,10},{19,3},{27,11},{20,4},{... | collective-permute-start | bytes 368648 | tf_op jit(solution)/shard_map/ppermute | solution.py:419

commit v2 on v1

--- a/solution.py
+++ b/solution.py
@@ -59,6 +59,7 @@
             shape(self.devices, 1, self.width, dtype=jnp.int32),
             [SMEM, SMEM],
             VMEM,
+            mib=63,
         )(source_slot, neighbours)
         return lax.all_to_all(sent, ("gx", "gy"), 0, 0, tiled=True)
 
@@ -301,11 +302,23 @@
             pl.when(kind == c)(functools.partial(prepare, lambda s, x, src=src: src[s, x]))
 
 
+def stencil():
+    source = lax.broadcasted_iota(jnp.int32, (256, 128), 0)
+    target = lax.broadcasted_iota(jnp.int32, (256, 128), 1)
+    inside = source < 128
+    step = jnp.abs(source - target)
+    along_z = (step == 1) & (source // B == target // B)
+    across = jnp.abs(source - 128 - target) == 128 - B
+    hit = (inside & (along_z | (step == B))) | (jnp.logical_not(inside) & across)
+    return jnp.where(hit, 1.0, 0.0).astype(jnp.bfloat16)
+
+
 def sweep_kernel(
     patches, plan, grid, fixed, factor, ghosts, g_ym, g_yp, g_xm, g_xp, g_y2m, g_y2p, blank,
-    out_ref, ghost, mid, base, stage, sems,
+    out_ref, ghost, mid_0, mid_1, base_0, base_1, weights, stage, sems,
 ):
     del blank
+    mids, bases = (mid_0, mid_1), (base_0, base_1)
     sub, lane = iotas()
     z = lane & (B - 1)
     z_low, z_high = z == 0, z == B - 1
@@ -313,10 +326,12 @@
     y_high = (sub == TILES - 1) & (lane >= 128 - B)
     zero = jnp.zeros(LAYER, F32)
     stage_rows = raw_rows(stage)
+    weights[...] = stencil()
 
     def clear_pad(i, carry):
-        for a in range(2):
-            mid[a, pl.ds(pl.multiple_of(i * PAD, 8), TILES), :] = zero
+        for mid in mids:
+            for a in range(2):
+                mid[a, pl.ds(pl.multiple_of(i * PAD, 8), TILES), :] = zero
         return carry
 
     lax.fori_loop(0, B + 1, clear_pad, 0, unroll=3)
@@ -337,7 +352,7 @@
             for c, src in enumerate((ghosts, g_ym, g_yp, g_xm, g_xp, g_y2m, g_y2p)):
                 pl.when(kind == c)(functools.partial(copy_face, ghost, t * SIDES + f, src, place))
 
-    def one_patch(t, s):
+    def add_ghosts(t, s):
         at_side = t * SIDES
         y_first, y_last = ghost[at_side + 2, s], ghost[at_side + 3, s]
         z_first, z_last = ghost[at_side + 4, s], ghost[at_side + 5, s]
@@ -355,44 +370,65 @@
                 outer = outer + ghost[at_side, s]
             if x == B - 1:
                 outer = outer + ghost[at_side + 1, s]
-            base[x] = fixed[t, s, x] + factor[t, s, x] * outer
-        for sweep in range(SWEEPS):
-
-            def load(row, sweep=sweep):
-                if sweep == 0:
-                    return grid[t, s, pl.ds(row, TILES), :]
-                return mid[(sweep - 1) % 2, pl.ds(row, TILES), :]
-
-            before = None
-            here = load(TILES)
-            for x in range(B):
-                at = x * PAD + TILES
-                after = load(at + PAD) if x < B - 1 else None
-                total = pltpu.roll(jnp.where(lane >= 128 - B, load(at - 1), here), B, 1)
-                total = total + pltpu.roll(jnp.where(lane < B, load(at + 1), here), 128 - B, 1)
-                total = total + jnp.where(z_low, zero, pltpu.roll(here, 1, 1))
-                total = total + jnp.where(z_high, zero, pltpu.roll(here, 127, 1))
-                if before is not None:
-                    total = total + before
-                if after is not None:
-                    total = total + after
-                new = base[x] + factor[t, s, x] * total
-                if sweep < SWEEPS - 1:
-                    mid[sweep % 2, pl.ds(at, TILES), :] = new
-                else:
-                    stage_rows[pl.ds(s * PER_S + x * PER_X + t, TILES, stride=8), :] = new
-                before, here = here, after
+            bases[t][x] = fixed[t, s, x] + factor[t, s, x] * outer
+
+    def loader(t, s, sweep):
+        def load(row):
+            if sweep == 0:
+                return grid[t, s, pl.ds(row, TILES), :]
+            return mids[t][(sweep - 1) % 2, pl.ds(row, TILES), :]
+
+        return load
+
+    def by_matmul(load):
+        layers = []
+        for x in range(B):
+            at = x * PAD + TILES
+            other = jnp.where(lane >= 64, load(at - 1), load(at + 1))
+            layers.append(jnp.concatenate([load(at), other], axis=1))
+        whole = jnp.concatenate(layers, axis=0)
+        high = whole.astype(jnp.bfloat16)
+        low = (whole - high.astype(F32)).astype(jnp.bfloat16)
+        w = weights[...]
+        sums = jnp.dot(high, w, preferred_element_type=F32)
+        sums = sums + jnp.dot(low, w, preferred_element_type=F32)
+        return [sums[x * TILES : (x + 1) * TILES] for x in range(B)]
+
+    def by_rolls(load, x, here):
+        at = x * PAD + TILES
+        total = pltpu.roll(jnp.where(lane >= 128 - B, load(at - 1), here), B, 1)
+        total = total + pltpu.roll(jnp.where(lane < B, load(at + 1), here), 128 - B, 1)
+        total = total + jnp.where(z_low, zero, pltpu.roll(here, 1, 1))
+        return total + jnp.where(z_high, zero, pltpu.roll(here, 127, 1))
+
+    def one_sweep(t, s, sweep, sums, live):
+        load = loader(t, s, sweep)
+        before, here = None, load(TILES)
+        for x in range(B):
+            at = x * PAD + TILES
+            after = load(at + PAD) if x < B - 1 else None
+            total = by_rolls(load, x, here) if sums is None else sums[x]
+            if before is not None:
+                total = total + before
+            if after is not None:
+                total = total + after
+            new = bases[t][x] + factor[t, s, x] * total
+            if sweep < SWEEPS - 1:
+                mids[t][sweep % 2, pl.ds(at, TILES), :] = new
+            else:
+                row = s * PER_S + x * PER_X + t
+                stage_rows[pl.ds(row, TILES, stride=8), :] = jnp.where(live, new, zero)
+            before, here = here, after
+
+    lives = [jnp.full(LAYER, patches[t], jnp.int32) >= 0 for t in range(WORKING)]
 
     def species(s, carry):
         for t in range(WORKING):
-            live = patches[t] >= 0
-            pl.when(live)(functools.partial(one_patch, t, s))
-
-            @pl.when(jnp.logical_not(live))
-            def _(t=t):
-                for x in range(B):
-                    stage_rows[pl.ds(s * PER_S + x * PER_X + t, TILES, stride=8), :] = zero
-
+            add_ghosts(t, s)
+        for sweep in range(SWEEPS):
+            for t in range(WORKING):
+                sums = by_matmul(loader(t, s, sweep)) if t % 2 else None
+                one_sweep(t, s, sweep, sums, lives[t])
         copy_out(s).start()
         return carry
 
@@ -517,7 +553,10 @@
         [
             pltpu.VMEM((WORKING * SIDES, species, *LAYER), F32),
             pltpu.VMEM((2, B * PAD + TILES, 128), F32),
+            pltpu.VMEM((2, B * PAD + TILES, 128), F32),
             pltpu.VMEM((B, *LAYER), F32),
+            pltpu.VMEM((B, *LAYER), F32),
+            pltpu.VMEM((256, 128), jnp.bfloat16),
             pltpu.VMEM((species, tiles, 8, 128), F32),
             pltpu.SemaphoreType.DMA((species,)),
         ],

time: 93.4 us -> 92 us (0.985)
  the two profiles are of different devices: /device:TPU:6 before, /device:TPU:0 now
where the time goes in v2:
time: 92 us; the launch traced here: 91.4 us
  starting transfers between devices  44.9 us (49%)
  Pallas kernels  25.1 us (27%)
  waiting for transfers between devices  20 us (22%)
  local copies, waits for them, and re-layouts  1.14 us (1%)
    ppermute x12, starting transfers between devices, passed_along(): return lax.ppermute(x, axis, pairs)  35.7 us
    pallas_call x8, Pallas kernels, run(): pl.pallas_call(kernel, out_shape=out_shape, in_specs=in_specs, out_specs=...  25.1 us
    ppermute x12, waiting for transfers between devices, passed_along(): return lax.ppermute(x, axis, pairs)  12.8 us
    all_to_all x1, starting transfers between devices, gather(): return lax.all_to_all(sent, ('gx', 'gy'), 0, 0, tiled=True)  9.15 us
    all_to_all x1, waiting for transfers between devices, gather(): return lax.all_to_all(sent, ('gx', 'gy'), 0, 0, tiled=True)  7.13 us
  transfers between devices with their start and end apart: 13, of which 3 were waited for; matrix products, arithmetic and copies ran while one was open for 0% of the time, Pallas kernels for 15%

profile of v2, /device:TPU:0, one launch (start us, length us, event | category | flops | bytes accessed | tf_op | source)
XLA Modules:
  0.0 91.4 jit_solution(16134746272787960182)
XLA Ops:
  0.0 5.5 %shard_map.65 = (f32[24,5,32,8,128]{4,3,2,1,0:T(8,128)}, f32[36,5,8,128]{3,2,1,0:T(8,128)}) custom-call(f32[5,256,6,128]{3,2,1,0:T(8,128)} %bitcast.7), custom_call_target="tpu_custom_call" | custom-call | tf_op jit(solution)/shard_map/pallas_call | solution.py:464
  5.5 2.4 %collective-permute-start = (f32[36,5,8,128]{3,2,1,0:T(8,128)}, f32[36,5,8,128]{3,2,1,0:T(8,128)S(1)}, u32[]{:S(2)}, u32[]{:S(2)}) collective-permute-start(f32[36,5,8,128]{3,2,1,0:T(8,128)} %get-tuple-element.25.faces.f_own), channel_id=1, source_target_pairs={{0,8},{8,16},{16,24},{1,9},{9,17},{17,25},{2,10},{10,18},{18,26},{... | collective-permute-start | bytes 2211848 | tf_op jit(solution)/shard_map/ppermute | solution.py:455
  8.0 1.3 %collective-permute-start.1 = (f32[36,5,8,128]{3,2,1,0:T(8,128)}, f32[36,5,8,128]{3,2,1,0:T(8,128)}, u32[]{:S(2)}, u32[]{:S(2)}) collective-permute-start(f32[36,5,8,128]{3,2,1,0:T(8,128)} %get-tuple-element.25.faces.f_own), channel_id=1, source_target_pairs={{8,0},{16,8},{24,16},{9,1},{17,9},{25,17},{10,2},{18,10},{26,18},{... | collective-permute-start | bytes 2211848 | tf_op jit(solution)/shard_map/ppermute | solution.py:455
  9.3 1.4 %shard_map.64 = s32[32,1,48]{2,1,0:T(1,128)} custom-call(s32[6]{0:T(128)} %source_slot.1, s32[6,6]{1,0:T(8,128)} %neighbours.1), custom_call_target="tpu_custom_call" | custom-call | tf_op jit(solution)/shard_map/pallas_call | solution.py:464
  10.6 9.2 %all-to-all-start = ((s32[32,1,48]{2,1,0:T(1,128)}), s32[32,1,48]{2,1,0:T(1,128)S(1)}, u32[]{:S(2)}, u32[]{:S(2)}) async-start(s32[32,1,48]{2,1,0:T(1,128)} %shard_map.64), calls=%async_computation | async-start | bytes 32768 | tf_op jit(solution)/shard_map/all_to_all | solution.py:64
  19.8 7.1 %all-to-all-done.table = s32[32,1,48]{2,1,0:T(1,128)S(1)} async-done(((s32[32,1,48]{2,1,0:T(1,128)}), s32[32,1,48]{2,1,0:T(1,128)S(1)}, u32[]{:S(2)}, u32[]{:S(2)}) %all-to-all-start) | async-done | bytes 6176 | tf_op jit(solution)/shard_map/all_to_all | solution.py:64
  26.9 0.0 copy-start
  26.9 1.1 %copy-done = f32[36,5,8,128]{3,2,1,0:T(8,128)S(1)} copy-done((f32[36,5,8,128]{3,2,1,0:T(8,128)S(1)}, f32[36,5,8,128]{3,2,1,0:T(8,128)}, u32[]{:S(2)}) %copy-start) | copy-done | bytes 737304
  28.0 3.1 %shard_map.66 = (f32[5,32,8,128]{3,2,1,0:T(8,128)S(1)}, f32[5,32,8,128]{3,2,1,0:T(8,128)S(1)}, f32[6,5,8,128]{3,2,1,0:T(8,128)S(1)}, f32[6,5,8,128]{3,2,1,0:T(8,...) custom-call(s32[1]{0:T(128)} %bitcast.me_ref, ...), custom_call_target="tpu_custom_call" | custom-call | tf_op jit(solution)/shard_map/pallas_call | solution.py:464
  31.2 1.8 %collective-permute-start.2 = (f32[5,32,8,128]{3,2,1,0:T(8,128)S(1)}, f32[5,32,8,128]{3,2,1,0:T(8,128)S(1)}, u32[]{:S(2)}, u32[]{:S(2)}) collective-permute-start(f32[5,32,8,128]{3,2,1,0:T(8,128)S(1)} %get-tuple-element.29), channel_id=1, source_target_pairs={{0,8},{8,16},{16,24},{1,9},{9,17},{17,25},{2,10},{10,18},{18,26},{... | collective-permute-start | bytes 1966088 | tf_op jit(solution)/shard_map/ppermute | solution.py:455
  33.0 0.0 copy-start.1
  33.0 1.4 %collective-permute-start.3 = (f32[5,32,8,128]{3,2,1,0:T(8,128)S(1)}, f32[5,32,8,128]{3,2,1,0:T(8,128)S(1)}, u32[]{:S(2)}, u32[]{:S(2)}) collective-permute-start(f32[5,32,8,128]{3,2,1,0:T(8,128)S(1)} %get-tuple-element.30), channel_id=1, source_target_pairs={{8,0},{16,8},{24,16},{9,1},{17,9},{25,17},{10,2},{18,10},{26,18},{... | collective-permute-start | bytes 1966088 | tf_op jit(solution)/shard_map/ppermute | solution.py:455
  34.4 2.1 %shard_map.68 = (f32[5,32,8,128]{3,2,1,0:T(8,128)S(1)}, f32[5,32,8,128]{3,2,1,0:T(8,128)S(1)}) custom-call(s32[1]{0:T(128)} %bitcast.me_ref, s32[32,1,48]{2,1,0:T(1,128)S(1)} %all-to-all-done.table, f32[24,5,32,8,128]{4,3,2,1,0:T(8,128)} %get-tuple-element.24.dense), custom_call_target="tpu_custom_call" | custom-call | tf_op jit(solution)/shard_map/pallas_call | solution.py:464
  36.5 0.0 copy-start.2
  36.5 0.0 copy-start.3
  36.6 0.0 copy-start.4
  36.6 2.9 %collective-permute-start.4 = (f32[5,32,8,128]{3,2,1,0:T(8,128)S(1)}, f32[5,32,8,128]{3,2,1,0:T(8,128)S(1)}, u32[]{:S(2)}, u32[]{:S(2)}) collective-permute-start(f32[5,32,8,128]{3,2,1,0:T(8,128)S(1)} %get-tuple-element.31), channel_id=1, source_target_pairs={{0,1},{1,2},{2,3},{3,4},{4,5},{5,6},{6,7},{8,9},{9,10},{10,11},{11... | collective-permute-start | bytes 1966088 | tf_op jit(solution)/shard_map/ppermute | solution.py:455
  39.5 0.0 collective-permute-done.f_xm
  39.5 1.3 %collective-permute-start.5 = (f32[5,32,8,128]{3,2,1,0:T(8,128)S(1)}, f32[5,32,8,128]{3,2,1,0:T(8,128)S(1)}, u32[]{:S(2)}, u32[]{:S(2)}) collective-permute-start(f32[5,32,8,128]{3,2,1,0:T(8,128)S(1)} %get-tuple-element.32), channel_id=1, source_target_pairs={{1,0},{2,1},{3,2},{4,3},{5,4},{6,5},{7,6},{9,8},{10,9},{11,10},{12... | collective-permute-start | bytes 1966088 | tf_op jit(solution)/shard_map/ppermute | solution.py:455
  40.8 0.0 collective-permute-done.1.f_xp
  40.8 5.3 %collective-permute-start.10 = (f32[6,5,8,128]{3,2,1,0:T(8,128)S(1)}, f32[6,5,8,128]{3,2,1,0:T(8,128)S(1)}, u32[]{:S(2)}, u32[]{:S(2)}) collective-permute-start(f32[6,5,8,128]{3,2,1,0:T(8,128)S(1)} %get-tuple-element.41), channel_id=1, source_target_pairs={{0,2},{1,3},{2,4},{3,5},{4,6},{5,7},{8,10},{9,11},{10,12},{11,13},... | collective-permute-start | bytes 368648 | tf_op jit(solution)/shard_map/ppermute | solution.py:455
  46.1 0.0 copy-done.1
  46.1 3.7 %shard_map.67 = (f32[12,5,8,128]{3,2,1,0:T(8,128)S(1)}, f32[12,5,8,128]{3,2,1,0:T(8,128)S(1)}, f32[12,5,8,128]{3,2,1,0:T(8,128)S(1)}, s32[24]{0:T(128)S(1)}) custom-call(s32[1]{0:T(128)} %bitcast.me_ref, s32[32,1,48]{2,1,0:T(1,128)S(1)} %all-to-all-done.table, f32[36,5,8,128]{3,2,1,0:T(8,128)S(1)} %copy-done.1, ...), custom_call_target="tpu_custom_call" | custom-call | tf_op jit(solution)/shard_map/pallas_call | solution.py:464
  49.8 0.0 collective-permute-done.10.g_y2m
  49.8 10.3 %collective-permute-start.6 = (f32[12,5,8,128]{3,2,1,0:T(8,128)S(1)}, f32[12,5,8,128]{3,2,1,0:T(8,128)S(1)}, u32[]{:S(2)}, u32[]{:S(2)}) collective-permute-start(f32[12,5,8,128]{3,2,1,0:T(8,128)S(1)} %get-tuple-element.37), channel_id=1, source_target_pairs={{0,1},{1,2},{2,3},{3,4},{4,5},{5,6},{6,7},{8,9},{9,10},{10,11},{11... | collective-permute-start | bytes 737288 | tf_op jit(solution)/shard_map/ppermute | solution.py:455
  60.2 0.0 collective-permute-done.2.p_xm
  60.2 1.3 %collective-permute-start.7 = (f32[12,5,8,128]{3,2,1,0:T(8,128)S(1)}, f32[12,5,8,128]{3,2,1,0:T(8,128)S(1)}, u32[]{:S(2)}, u32[]{:S(2)}) collective-permute-start(f32[12,5,8,128]{3,2,1,0:T(8,128)S(1)} %get-tuple-element.38), channel_id=1, source_target_pairs={{1,0},{2,1},{3,2},{4,3},{5,4},{6,5},{7,6},{9,8},{10,9},{11,10},{12... | collective-permute-start | bytes 737288 | tf_op jit(solution)/shard_map/ppermute | solution.py:455
  61.5 0.0 collective-permute-done.3.p_xp
  61.5 1.3 %collective-permute-start.11 = (f32[6,5,8,128]{3,2,1,0:T(8,128)S(1)}, f32[6,5,8,128]{3,2,1,0:T(8,128)S(1)}, u32[]{:S(2)}, u32[]{:S(2)}) collective-permute-start(f32[6,5,8,128]{3,2,1,0:T(8,128)S(1)} %get-tuple-element.42), channel_id=1, source_target_pairs={{2,0},{3,1},{4,2},{5,3},{6,4},{7,5},{10,8},{11,9},{12,10},{13,11},... | collective-permute-start | bytes 368648 | tf_op jit(solution)/shard_map/ppermute | solution.py:455
  62.8 10.8 %collective-permute-done.4.p_ym = f32[5,32,8,128]{3,2,1,0:T(8,128)S(1)} collective-permute-done((f32[5,32,8,128]{3,2,1,0:T(8,128)S(1)}, f32[5,32,8,128]{3,2,1,0:T(8,128)S(1)}, u32[]{:S(2)}, u32[]{:S(2)}) %collective-permute-start.4) | collective-permute-done | bytes 655392 | tf_op jit(solution)/shard_map/ppermute | solution.py:455
  73.6 5.1 %collective-permute-start.8 = (f32[6,5,8,128]{3,2,1,0:T(8,128)S(1)}, f32[6,5,8,128]{3,2,1,0:T(8,128)S(1)}, u32[]{:S(2)}, u32[]{:S(2)}) collective-permute-start(f32[6,5,8,128]{3,2,1,0:T(8,128)S(1)} %get-tuple-element.39), channel_id=1, source_target_pairs={{0,16},{8,24},{1,17},{9,25},{2,18},{10,26},{3,19},{11,27},{4,20},{... | collective-permute-start | bytes 368648 | tf_op jit(solution)/shard_map/ppermute | solution.py:455
  78.7 0.0 collective-permute-done.5.p_yp
  78.7 1.3 %collective-permute-start.9 = (f32[6,5,8,128]{3,2,1,0:T(8,128)S(1)}, f32[6,5,8,128]{3,2,1,0:T(8,128)S(1)}, u32[]{:S(2)}, u32[]{:S(2)}) collective-permute-start(f32[6,5,8,128]{3,2,1,0:T(8,128)S(1)} %get-tuple-element.40), channel_id=1, source_target_pairs={{16,0},{24,8},{17,1},{25,9},{18,2},{26,10},{19,3},{27,11},{20,4},{... | collective-permute-start | bytes 368648 | tf_op jit(solution)/shard_map/ppermute | solution.py:455
  80.0 2.0 %shard_map.70.blank = f32[5,256,6,128]{3,2,1,0:T(8,128)} custom-call(), custom_call_target="tpu_custom_call" | custom-call | tf_op jit(solution)/shard_map/pallas_call | solution.py:464
  82.0 0.0 copy-done.2
  82.0 0.0 copy-done.3
  82.0 0.0 copy-done.4
  82.0 1.4 %shard_map.69 = (f32[2,5,520,128]{3,2,1,0:T(8,128)S(1)}, f32[2,5,32,8,128]{4,3,2,1,0:T(8,128)S(1)}, f32[2,5,32,8,128]{4,3,2,1,0:T(8,128)S(1)}) custom-call(s32[2]{0:T(128)S(1)} %get-tuple-element.26.patches, f32[5]{0:T(128)S(1)} %copy-done.2, f32[5]{0:T(128)S(1)} %copy-done.3, f32[5]{0:T(128)S(1)} %copy-done.4, ...), custom_call_target="tpu_custom_call" | custom-call | tf_op jit(solution)/shard_map/pallas_call | solution.py:464
  83.4 0.0 collective-permute-done.11.g_y2p
  83.5 0.0 collective-permute-done.8.g_xm
  83.5 2.0 %collective-permute-done.9.g_xp = f32[6,5,8,128]{3,2,1,0:T(8,128)S(1)} collective-permute-done((f32[6,5,8,128]{3,2,1,0:T(8,128)S(1)}, f32[6,5,8,128]{3,2,1,0:T(8,128)S(1)}, u32[]{:S(2)}, u32[]{:S(2)}) %collective-permute-start.9) | collective-permute-done | bytes 122912 | tf_op jit(solution)/shard_map/ppermute | solution.py:455
  85.5 0.0 collective-permute-done.6.g_ym
  85.5 0.0 collective-permute-done.7.g_yp
  85.5 5.9 %shard_map.71 = f32[5,256,6,128]{3,2,1,0:T(8,128)} custom-call(s32[2]{0:T(128)S(1)} %get-tuple-element.26.patches, s32[24]{0:T(128)S(1)} %get-tuple-element.27.plan, f32[2,5,520,128]{3,2,1,0:T(8,128)S(1)} %get-tuple-element.33.grid, f32[2,5,32,8,128]{4,3,2,1,0:T(8,128)S(1)} %get-tuple-element.34.fixed, ...), custom_call_target="tpu_custom_call", output_to_operand_aliasing={{}: (12, {})} | custom-call | tf_op jit(solution)/shard_map/pallas_call | solution.py:464
Async XLA Ops:
  5.5 34.0 %collective-permute-start = (f32[36,5,8,128]{3,2,1,0:T(8,128)}, f32[36,5,8,128]{3,2,1,0:T(8,128)S(1)}, u32[]{:S(2)}, u32[]{:S(2)}) collective-permute-start(f32[36,5,8,128]{3,2,1,0:T(8,128)} %get-tuple-element.25.faces.f_own), channel_id=1, source_target_pairs={{0,8},{8,16},{16,24},{1,9},{9,17},{17,25},{2,10},{10,18},{18,26},{... | collective-permute-start | bytes 2211848 | tf_op jit(solution)/shard_map/ppermute | solution.py:455
  8.0 32.9 %collective-permute-start.1 = (f32[36,5,8,128]{3,2,1,0:T(8,128)}, f32[36,5,8,128]{3,2,1,0:T(8,128)}, u32[]{:S(2)}, u32[]{:S(2)}) collective-permute-start(f32[36,5,8,128]{3,2,1,0:T(8,128)} %get-tuple-element.25.faces.f_own), channel_id=1, source_target_pairs={{8,0},{16,8},{24,16},{9,1},{17,9},{25,17},{10,2},{18,10},{26,18},{... | collective-permute-start | bytes 2211848 | tf_op jit(solution)/shard_map/ppermute | solution.py:455
  10.6 16.3 %all-to-all-start = ((s32[32,1,48]{2,1,0:T(1,128)}), s32[32,1,48]{2,1,0:T(1,128)S(1)}, u32[]{:S(2)}, u32[]{:S(2)}) async-start(s32[32,1,48]{2,1,0:T(1,128)} %shard_map.64), calls=%async_computation | async-start | bytes 32768 | tf_op jit(solution)/shard_map/all_to_all | solution.py:64
  26.9 1.1 %copy-start = (f32[36,5,8,128]{3,2,1,0:T(8,128)S(1)}, f32[36,5,8,128]{3,2,1,0:T(8,128)}, u32[]{:S(2)}) copy-start(f32[36,5,8,128]{3,2,1,0:T(8,128)} %get-tuple-element.25.faces.f_own) | copy-start | bytes 2211844
  31.2 29.0 %collective-permute-start.2 = (f32[5,32,8,128]{3,2,1,0:T(8,128)S(1)}, f32[5,32,8,128]{3,2,1,0:T(8,128)S(1)}, u32[]{:S(2)}, u32[]{:S(2)}) collective-permute-start(f32[5,32,8,128]{3,2,1,0:T(8,128)S(1)} %get-tuple-element.29), channel_id=1, source_target_pairs={{0,8},{8,16},{16,24},{1,9},{9,17},{17,25},{2,10},{10,18},{18,26},{... | collective-permute-start | bytes 1966088 | tf_op jit(solution)/shard_map/ppermute | solution.py:455
  33.0 13.2 %copy-start.1 = (f32[36,5,8,128]{3,2,1,0:T(8,128)S(1)}, f32[36,5,8,128]{3,2,1,0:T(8,128)}, u32[]{:S(2)}) copy-start(f32[36,5,8,128]{3,2,1,0:T(8,128)} %get-tuple-element.25.faces.f_own) | copy-start | bytes 2211844
  33.0 28.5 %collective-permute-start.3 = (f32[5,32,8,128]{3,2,1,0:T(8,128)S(1)}, f32[5,32,8,128]{3,2,1,0:T(8,128)S(1)}, u32[]{:S(2)}, u32[]{:S(2)}) collective-permute-start(f32[5,32,8,128]{3,2,1,0:T(8,128)S(1)} %get-tuple-element.30), channel_id=1, source_target_pairs={{8,0},{16,8},{24,16},{9,1},{17,9},{25,17},{10,2},{18,10},{26,18},{... | collective-permute-start | bytes 1966088 | tf_op jit(solution)/shard_map/ppermute | solution.py:455
  36.5 45.5 %copy-start.2 = (f32[5]{0:T(128)S(1)}, f32[5]{0:T(128)}, u32[]{:S(2)}) copy-start(f32[5]{0:T(128)} %mob.1) | copy-start | bytes 64
  36.5 45.5 %copy-start.3 = (f32[5]{0:T(128)S(1)}, f32[5]{0:T(128)}, u32[]{:S(2)}) copy-start(f32[5]{0:T(128)} %gain.1) | copy-start | bytes 64
  36.6 45.5 %copy-start.4 = (f32[5]{0:T(128)S(1)}, f32[5]{0:T(128)}, u32[]{:S(2)}) copy-start(f32[5]{0:T(128)} %rates.1) | copy-start | bytes 64
  36.6 37.0 %collective-permute-start.4 = (f32[5,32,8,128]{3,2,1,0:T(8,128)S(1)}, f32[5,32,8,128]{3,2,1,0:T(8,128)S(1)}, u32[]{:S(2)}, u32[]{:S(2)}) collective-permute-start(f32[5,32,8,128]{3,2,1,0:T(8,128)S(1)} %get-tuple-element.31), channel_id=1, source_target_pairs={{0,1},{1,2},{2,3},{3,4},{4,5},{5,6},{6,7},{8,9},{9,10},{10,11},{11... | collective-permute-start | bytes 1966088 | tf_op jit(solution)/shard_map/ppermute | solution.py:455
  39.5 39.2 %collective-permute-start.5 = (f32[5,32,8,128]{3,2,1,0:T(8,128)S(1)}, f32[5,32,8,128]{3,2,1,0:T(8,128)S(1)}, u32[]{:S(2)}, u32[]{:S(2)}) collective-permute-start(f32[5,32,8,128]{3,2,1,0:T(8,128)S(1)} %get-tuple-element.32), channel_id=1, source_target_pairs={{1,0},{2,1},{3,2},{4,3},{5,4},{6,5},{7,6},{9,8},{10,9},{11,10},{12... | collective-permute-start | bytes 1966088 | tf_op jit(solution)/shard_map/ppermute | solution.py:455
  40.8 9.0 %collective-permute-start.10 = (f32[6,5,8,128]{3,2,1,0:T(8,128)S(1)}, f32[6,5,8,128]{3,2,1,0:T(8,128)S(1)}, u32[]{:S(2)}, u32[]{:S(2)}) collective-permute-start(f32[6,5,8,128]{3,2,1,0:T(8,128)S(1)} %get-tuple-element.41), channel_id=1, source_target_pairs={{0,2},{1,3},{2,4},{3,5},{4,6},{5,7},{8,10},{9,11},{10,12},{11,13},... | collective-permute-start | bytes 368648 | tf_op jit(solution)/shard_map/ppermute | solution.py:455
  49.8 35.6 %collective-permute-start.6 = (f32[12,5,8,128]{3,2,1,0:T(8,128)S(1)}, f32[12,5,8,128]{3,2,1,0:T(8,128)S(1)}, u32[]{:S(2)}, u32[]{:S(2)}) collective-permute-start(f32[12,5,8,128]{3,2,1,0:T(8,128)S(1)} %get-tuple-element.37), channel_id=1, source_target_pairs={{0,1},{1,2},{2,3},{3,4},{4,5},{5,6},{6,7},{8,9},{9,10},{10,11},{11... | collective-permute-start | bytes 737288 | tf_op jit(solution)/shard_map/ppermute | solution.py:455
  60.2 25.3 %collective-permute-start.7 = (f32[12,5,8,128]{3,2,1,0:T(8,128)S(1)}, f32[12,5,8,128]{3,2,1,0:T(8,128)S(1)}, u32[]{:S(2)}, u32[]{:S(2)}) collective-permute-start(f32[12,5,8,128]{3,2,1,0:T(8,128)S(1)} %get-tuple-element.38), channel_id=1, source_target_pairs={{1,0},{2,1},{3,2},{4,3},{5,4},{6,5},{7,6},{9,8},{10,9},{11,10},{12... | collective-permute-start | bytes 737288 | tf_op jit(solution)/shard_map/ppermute | solution.py:455
  61.5 22.0 %collective-permute-start.11 = (f32[6,5,8,128]{3,2,1,0:T(8,128)S(1)}, f32[6,5,8,128]{3,2,1,0:T(8,128)S(1)}, u32[]{:S(2)}, u32[]{:S(2)}) collective-permute-start(f32[6,5,8,128]{3,2,1,0:T(8,128)S(1)} %get-tuple-element.42), channel_id=1, source_target_pairs={{2,0},{3,1},{4,2},{5,3},{6,4},{7,5},{10,8},{11,9},{12,10},{13,11},... | collective-permute-start | bytes 368648 | tf_op jit(solution)/shard_map/ppermute | solution.py:455
  73.6 9.9 %collective-permute-start.8 = (f32[6,5,8,128]{3,2,1,0:T(8,128)S(1)}, f32[6,5,8,128]{3,2,1,0:T(8,128)S(1)}, u32[]{:S(2)}, u32[]{:S(2)}) collective-permute-start(f32[6,5,8,128]{3,2,1,0:T(8,128)S(1)} %get-tuple-element.39), channel_id=1, source_target_pairs={{0,16},{8,24},{1,17},{9,25},{2,18},{10,26},{3,19},{11,27},{4,20},{... | collective-permute-start | bytes 368648 | tf_op jit(solution)/shard_map/ppermute | solution.py:455
  78.7 6.8 %collective-permute-start.9 = (f32[6,5,8,128]{3,2,1,0:T(8,128)S(1)}, f32[6,5,8,128]{3,2,1,0:T(8,128)S(1)}, u32[]{:S(2)}, u32[]{:S(2)}) collective-permute-start(f32[6,5,8,128]{3,2,1,0:T(8,128)S(1)} %get-tuple-element.40), channel_id=1, source_target_pairs={{16,0},{24,8},{17,1},{25,9},{18,2},{26,10},{19,3},{27,11},{20,4},{... | collective-permute-start | bytes 368648 | tf_op jit(solution)/shard_map/ppermute | solution.py:455

commit v3 on v2

--- a/solution.py
+++ b/solution.py
@@ -184,10 +184,40 @@
         copy.wait()
 
 
-def second_kernel(
-    info, me_ref, table, dense, faces, to_xp, to_xm, to_x2p, to_x2m, to_y2p, to_y2m, own, patches,
-    sems,
-):
+def plan_sides(info, me, table, plan):
+    my_column = me // info.rows
+    my_row = me - my_column * info.rows
+    for t in range(WORKING):
+        slot = info.take(table, me, t)
+
+        @each_side
+        def _(f, t=t, slot=slot):
+            near, face = info.need(table, slot, f)
+            at = t * SIDES + f
+            safe = jnp.maximum(near, 0)
+            home = info.device(safe)
+            column = home // info.rows
+            row = home - column * info.rows
+            beside = jnp.abs(column - my_column) < 2
+            here = (safe - home * info.cap) * SIDES + face
+            kind, place = jnp.int32(0), here
+            for c, far in ((7, -info.rows), (8, info.rows)):
+                kind = jnp.where(home == me + far, c, kind)
+            for c, far in ((1, -1), (2, 1)):
+                hit = beside & (row == my_row + far)
+                kind, place = jnp.where(hit, c, kind), jnp.where(hit, at, place)
+            for c, far in ((3, -2 * info.rows), (4, 2 * info.rows)):
+                hit = home == me + far
+                kind, place = jnp.where(hit, c, kind), jnp.where(hit, f, place)
+            for c, far in ((5, -2), (6, 2)):
+                hit = (column == my_column) & (row == my_row + far)
+                kind, place = jnp.where(hit, c, kind), jnp.where(hit, f, place)
+            plan[at] = jnp.where(near >= 0, kind, 0)
+            plan[WORKING * SIDES + at] = jnp.where(near >= 0, place, 0)
+
+
+def second_kernel(info, me_ref, table, dense, faces, *refs):
+    to_xp, to_xm, to_x2p, to_x2m, to_y2p, to_y2m, own, sems = refs
     me = me_ref[0]
     up, down = picked(info, table, me, me + info.rows), picked(info, table, me, me - info.rows)
     kept = [info.local(info.take(table, me, t), me)[1] for t in range(WORKING)]
@@ -195,12 +225,6 @@
     copies = patch_copies(pairs, dense, sems)
     for copy in copies:
         copy.start()
-    for t in range(WORKING):
-        slot = info.take(table, me, t)
-        kind = jnp.int32(-1)
-        for c, device in enumerate((me, me - info.rows, me + info.rows, me - 1, me + 1)):
-            kind = jnp.where((slot >= 0) & info.local(slot, device)[0], c, kind)
-        patches[t] = kind
 
     for step, out in ((info.rows, to_x2p), (-info.rows, to_x2m), (1, to_y2p), (-1, to_y2m)):
         for t in range(WORKING):
@@ -221,42 +245,45 @@
         copy.wait()
 
 
-def faces_kernel(info, me_ref, table, f_own, f_xm, f_xp, to_yp, to_ym, ghosts, plan):
+def copy_row(info, me, near, face, out, at, f_own, f_xm, f_xp):
+    for shift, src in ((0, f_own), (-info.rows, f_xm), (info.rows, f_xp)):
+        here, number = info.local(near, me + shift)
+        pl.when((near >= 0) & here)(
+            functools.partial(copy_face, out, at, src, number * SIDES + face)
+        )
+
+
+def faces_kernel(info, me_ref, table, f_own, f_xm, f_xp, to_yp, to_ym):
     me = me_ref[0]
-    shifts = ((0, f_own), (-info.rows, f_xm), (info.rows, f_xp))
-    for step, out in ((1, to_yp), (-1, to_ym), (0, ghosts)):
+    for step, out in ((1, to_yp), (-1, to_ym)):
         for t in range(WORKING):
             slot = info.take(table, me + step, t)
 
             @each_side
-            def _(f, t=t, step=step, out=out, slot=slot):
+            def _(f, t=t, out=out, slot=slot):
                 near, face = info.need(table, slot, f)
-                at = t * SIDES + f
-                for shift, src in shifts:
-                    here, number = info.local(near, me + shift)
-                    pl.when((near >= 0) & here)(
-                        functools.partial(copy_face, out, at, src, number * SIDES + face)
-                    )
-                if step == 0:
-                    home = info.device(jnp.maximum(near, 0))
-                    column, my_column = home // info.rows, me // info.rows
-                    row, my_row = home - column * info.rows, me - my_column * info.rows
-                    beside = jnp.abs(column - my_column) < 2
-                    kind, place = jnp.int32(0), at
-                    kind = jnp.where(beside & (row == my_row - 1), 1, kind)
-                    kind = jnp.where(beside & (row == my_row + 1), 2, kind)
-                    for c, far in ((3, -2 * info.rows), (4, 2 * info.rows)):
-                        kind = jnp.where(home == me + far, c, kind)
-                    for c, far in ((5, -2), (6, 2)):
-                        kind = jnp.where((column == my_column) & (row == my_row + far), c, kind)
-                    place = jnp.where(kind > 2, f, place)
-                    plan[at] = jnp.where(near >= 0, kind, 0)
-                    plan[WORKING * SIDES + at] = place
+                copy_row(info, me, near, face, out, t * SIDES + f, f_own, f_xm, f_xp)
 
 
 def prepare_kernel(
-    patches, mob, gain, rates, own, p_xm, p_xp, p_ym, p_yp, grid, fixed, factor
+    info, me_ref, table, mob, gain, rates, own, p_xm, p_xp, p_ym, p_yp,
+    grid, fixed, factor, patches, plan, blank, zeros, sems,
 ):
+    zeros[...] = jnp.zeros(zeros.shape, F32)
+    copies = [
+        pltpu.make_async_copy(zeros.at[:, pl.ds(0, info.cap), :], blank.at[s], sems.at[s])
+        for s in range(SPECIES)
+    ]
+    for copy in copies:
+        copy.start()
+    me = me_ref[0]
+    for t in range(WORKING):
+        slot = info.take(table, me, t)
+        kind = jnp.int32(-1)
+        for c, device in enumerate((me, me - info.rows, me + info.rows, me - 1, me + 1)):
+            kind = jnp.where((slot >= 0) & info.local(slot, device)[0], c, kind)
+        patches[t] = kind
+    plan_sides(info, me, table, plan)
     zero = jnp.zeros(LAYER, F32)
 
     def full(value):
@@ -301,6 +328,9 @@
         for c, src in ((1, p_xm), (2, p_xp), (3, p_ym), (4, p_yp)):
             pl.when(kind == c)(functools.partial(prepare, lambda s, x, src=src: src[s, x]))
 
+    for copy in copies:
+        copy.wait()
+
 
 def stencil():
     source = lax.broadcasted_iota(jnp.int32, (256, 128), 0)
@@ -314,8 +344,8 @@
 
 
 def sweep_kernel(
-    patches, plan, grid, fixed, factor, ghosts, g_ym, g_yp, g_xm, g_xp, g_y2m, g_y2p, blank,
-    out_ref, ghost, mid_0, mid_1, base_0, base_1, weights, stage, sems,
+    patches, plan, grid, fixed, factor, f_own, f_xm, f_xp, g_ym, g_yp, g_xm, g_xp, g_y2m, g_y2p,
+    blank, out_ref, ghost, mid_0, mid_1, base_0, base_1, weights, stage, sems,
 ):
     del blank
     mids, bases = (mid_0, mid_1), (base_0, base_1)
@@ -349,7 +379,9 @@
         def _(f, t=t):
             kind = plan[t * SIDES + f]
             place = plan[WORKING * SIDES + t * SIDES + f]
-            for c, src in enumerate((ghosts, g_ym, g_yp, g_xm, g_xp, g_y2m, g_y2p)):
+            for c, src in enumerate(
+                (f_own, g_ym, g_yp, g_xm, g_xp, g_y2m, g_y2p, f_xm, f_xp)
+            ):
                 pl.when(kind == c)(functools.partial(copy_face, ghost, t * SIDES + f, src, place))
 
     def add_ghosts(t, s):
@@ -427,7 +459,7 @@
             add_ghosts(t, s)
         for sweep in range(SWEEPS):
             for t in range(WORKING):
-                sums = by_matmul(loader(t, s, sweep)) if t % 2 else None
+                sums = by_matmul(loader(t, s, sweep)) if t % 2 or sweep == 0 else None
                 one_sweep(t, s, sweep, sums, lives[t])
         copy_out(s).start()
         return carry
@@ -435,18 +467,6 @@
     lax.fori_loop(0, SPECIES, species, 0)
     for s in range(SPECIES):
         copy_out(s).wait()
-
-
-def blank_kernel(cap, out_ref, zeros, sems):
-    zeros[...] = jnp.zeros(zeros.shape, F32)
-
-    def copy(s):
-        return pltpu.make_async_copy(zeros.at[:, pl.ds(0, cap), :], out_ref.at[s], sems.at[s])
-
-    for s in range(SPECIES):
-        copy(s).start()
-    for s in range(SPECIES):
-        copy(s).wait()
 
 
 def passed_along(x, axis, by):
@@ -504,14 +524,6 @@
         ],
         mib=57,
     )(view)
-    blank = call(
-        functools.partial(blank_kernel, cap),
-        shape(species, tiles, cap, 128),
-        [],
-        ANY,
-        [pltpu.VMEM((tiles, 8, 128), F32), pltpu.SemaphoreType.DMA((species,))],
-    )()
-
     s_yp, s_ym = call(
         functools.partial(first_kernel, info), (patch,) * 2, [SMEM, SMEM, HBM], (VMEM,) * 2,
         [pltpu.SemaphoreType.DMA((2,))],
@@ -520,35 +532,47 @@
     p_ym, p_yp = both_ways(s_yp, s_ym, "gy", 1)
     f_xm, f_xp = both_ways(faces, faces, "gx", 1)
 
-    s_xp, s_xm, t_x2p, t_x2m, t_y2p, t_y2m, own, patches = call(
+    s_xp, s_xm, t_x2p, t_x2m, t_y2p, t_y2m, own = call(
         functools.partial(second_kernel, info),
-        (patch, patch) + (one_patch,) * 4 + (two_patches, shape(WORKING, dtype=jnp.int32)),
+        (patch, patch) + (one_patch,) * 4 + (two_patches,),
         [SMEM, SMEM, HBM, VMEM],
-        (VMEM,) * 7 + (SMEM,),
+        (VMEM,) * 7,
         [pltpu.SemaphoreType.DMA((2 + WORKING,))],
         mib=50,
     )(me, table, dense, faces)
     p_xm, p_xp = both_ways(s_xp, s_xm, "gx", 1)
 
-    t_yp, t_ym, ghosts, plan = call(
+    t_yp, t_ym = call(
         functools.partial(faces_kernel, info),
-        (all_sides,) * 3 + (shape(2 * WORKING * SIDES, dtype=jnp.int32),),
+        (all_sides,) * 2,
         [SMEM] * 2 + [VMEM] * 3,
-        (VMEM,) * 3 + (SMEM,),
+        (VMEM,) * 2,
     )(me, table, faces, f_xm, f_xp)
     g_ym, g_yp = both_ways(t_yp, t_ym, "gy", 1)
     g_y2m, g_y2p = both_ways(t_y2p, t_y2m, "gy", 2)
     g_x2m, g_x2p = both_ways(t_x2p, t_x2m, "gx", 2)
 
     padded = shape(WORKING, species, B * PAD + TILES, 128)
-    grid, fixed, factor = call(
-        prepare_kernel, (padded, two_patches, two_patches), [SMEM] * 4 + [VMEM] * 5, (VMEM,) * 3
-    )(patches, mobility, fermi_gain, rates, own, p_xm, p_xp, p_ym, p_yp)
+    grid, fixed, factor, patches, plan, blank = call(
+        functools.partial(prepare_kernel, info),
+        (
+            padded,
+            two_patches,
+            two_patches,
+            shape(WORKING, dtype=jnp.int32),
+            shape(2 * WORKING * SIDES, dtype=jnp.int32),
+            shape(species, tiles, cap, 128),
+        ),
+        [SMEM] * 5 + [VMEM] * 5,
+        (VMEM,) * 3 + (SMEM, SMEM, ANY),
+        [pltpu.VMEM((tiles, 8, 128), F32), pltpu.SemaphoreType.DMA((species,))],
+        mib=4,
+    )(me, table, mobility, fermi_gain, rates, own, p_xm, p_xp, p_ym, p_yp)
 
     moved = call(
         sweep_kernel,
         shape(species, tiles, cap, 128),
-        [SMEM] * 2 + [VMEM] * 10 + [ANY],
+        [SMEM] * 2 + [VMEM] * 12 + [ANY],
         ANY,
         [
             pltpu.VMEM((WORKING * SIDES, species, *LAYER), F32),
@@ -560,9 +584,12 @@
             pltpu.VMEM((species, tiles, 8, 128), F32),
             pltpu.SemaphoreType.DMA((species,)),
         ],
-        {12: 0},
+        {14: 0},
         mib=10,
-    )(patches, plan, grid, fixed, factor, ghosts, g_ym, g_yp, g_x2m, g_x2p, g_y2m, g_y2p, blank)
+    )(
+        patches, plan, grid, fixed, factor, faces, f_xm, f_xp,
+        g_ym, g_yp, g_x2m, g_x2p, g_y2m, g_y2p, blank,
+    )
     return moved.transpose(2, 0, 1, 3).reshape(cap, species, cells)
 
 

time: 92 us -> 91.4 us (level)
  Pallas kernels: 25.1 us -> 23.3 us
  waiting for transfers between devices: 20 us -> 21.1 us
    pallas_call x8 -> x7, Pallas kernels: 25.1 us -> 23.3 us  [run(): pl.pallas_call(kernel, out_shape=out_shape, in_specs=in_specs, out_specs=...]
    ppermute x12, waiting for transfers between devices: 12.8 us -> 13.9 us  [passed_along(): return lax.ppermute(x, axis, pairs)]
  transfers between devices with their start and end apart: 13 -> 13, of which waited for: 3 -> 4; matrix products, arithmetic and copies ran while one was open for 0% -> 0% of each run, Pallas kernels for 15% -> 13%
where the time goes in v3:
time: 91.4 us; the launch traced here: 90.7 us
  starting transfers between devices  45 us (49%)
  Pallas kernels  23.3 us (25%)
  waiting for transfers between devices  21.1 us (23%)
  local copies, waits for them, and re-layouts  1.14 us (1%)
    ppermute x12, starting transfers between devices, passed_along(): return lax.ppermute(x, axis, pairs)  35.8 us
    pallas_call x7, Pallas kernels, run(): pl.pallas_call(kernel, out_shape=out_shape, in_specs=in_specs, out_specs=...  23.3 us
    ppermute x12, waiting for transfers between devices, passed_along(): return lax.ppermute(x, axis, pairs)  13.9 us
    all_to_all x1, starting transfers between devices, gather(): return lax.all_to_all(sent, ('gx', 'gy'), 0, 0, tiled=True)  9.15 us
    all_to_all x1, waiting for transfers between devices, gather(): return lax.all_to_all(sent, ('gx', 'gy'), 0, 0, tiled=True)  7.13 us
  transfers between devices with their start and end apart: 13, of which 4 were waited for; matrix products, arithmetic and copies ran while one was open for 0% of the time, Pallas kernels for 13%

profile of v3, /device:TPU:0, one launch (start us, length us, event | category | flops | bytes accessed | tf_op | source)
XLA Modules:
  0.0 90.7 jit_solution(15776540759356661119)
XLA Ops:
  0.0 5.5 %shard_map.65 = (f32[24,5,32,8,128]{4,3,2,1,0:T(8,128)}, f32[36,5,8,128]{3,2,1,0:T(8,128)}) custom-call(f32[5,256,6,128]{3,2,1,0:T(8,128)} %bitcast.7), custom_call_target="tpu_custom_call" | custom-call | tf_op jit(solution)/shard_map/pallas_call | solution.py:484
  5.5 2.4 %collective-permute-start.4 = (f32[36,5,8,128]{3,2,1,0:T(8,128)}, f32[36,5,8,128]{3,2,1,0:T(8,128)S(1)}, u32[]{:S(2)}, u32[]{:S(2)}) collective-permute-start(f32[36,5,8,128]{3,2,1,0:T(8,128)} %get-tuple-element.25.faces.f_own), channel_id=1, source_target_pairs={{0,8},{8,16},{16,24},{1,9},{9,17},{17,25},{2,10},{10,18},{18,26},{... | collective-permute-start | bytes 2211848 | tf_op jit(solution)/shard_map/ppermute | solution.py:475
  7.9 1.3 %collective-permute-start.5 = (f32[36,5,8,128]{3,2,1,0:T(8,128)}, f32[36,5,8,128]{3,2,1,0:T(8,128)}, u32[]{:S(2)}, u32[]{:S(2)}) collective-permute-start(f32[36,5,8,128]{3,2,1,0:T(8,128)} %get-tuple-element.25.faces.f_own), channel_id=1, source_target_pairs={{8,0},{16,8},{24,16},{9,1},{17,9},{25,17},{10,2},{18,10},{26,18},{... | collective-permute-start | bytes 2211848 | tf_op jit(solution)/shard_map/ppermute | solution.py:475
  9.2 1.4 %shard_map.64 = s32[32,1,48]{2,1,0:T(1,128)} custom-call(s32[6]{0:T(128)} %source_slot.1, s32[6,6]{1,0:T(8,128)} %neighbours.1), custom_call_target="tpu_custom_call" | custom-call | tf_op jit(solution)/shard_map/pallas_call | solution.py:484
  10.6 9.2 %all-to-all-start = ((s32[32,1,48]{2,1,0:T(1,128)}), s32[32,1,48]{2,1,0:T(1,128)S(1)}, u32[]{:S(2)}, u32[]{:S(2)}) async-start(s32[32,1,48]{2,1,0:T(1,128)} %shard_map.64), calls=%async_computation | async-start | bytes 32768 | tf_op jit(solution)/shard_map/all_to_all | solution.py:64
  19.8 7.1 %all-to-all-done.table = s32[32,1,48]{2,1,0:T(1,128)S(1)} async-done(((s32[32,1,48]{2,1,0:T(1,128)}), s32[32,1,48]{2,1,0:T(1,128)S(1)}, u32[]{:S(2)}, u32[]{:S(2)}) %all-to-all-start) | async-done | bytes 6176 | tf_op jit(solution)/shard_map/all_to_all | solution.py:64
  26.9 0.0 copy-start
  26.9 1.1 %copy-done = f32[36,5,8,128]{3,2,1,0:T(8,128)S(1)} copy-done((f32[36,5,8,128]{3,2,1,0:T(8,128)S(1)}, f32[36,5,8,128]{3,2,1,0:T(8,128)}, u32[]{:S(2)}) %copy-start) | copy-done | bytes 737304
  28.0 2.5 %shard_map.66 = (f32[5,32,8,128]{3,2,1,0:T(8,128)S(1)}, f32[5,32,8,128]{3,2,1,0:T(8,128)S(1)}, f32[6,5,8,128]{3,2,1,0:T(8,128)S(1)}, f32[6,5,8,128]{3,2,1,0:T(8,...) custom-call(s32[1]{0:T(128)} %bitcast.me_ref, ...), custom_call_target="tpu_custom_call" | custom-call | tf_op jit(solution)/shard_map/pallas_call | solution.py:484
  30.6 1.8 %collective-permute-start = (f32[5,32,8,128]{3,2,1,0:T(8,128)S(1)}, f32[5,32,8,128]{3,2,1,0:T(8,128)S(1)}, u32[]{:S(2)}, u32[]{:S(2)}) collective-permute-start(f32[5,32,8,128]{3,2,1,0:T(8,128)S(1)} %get-tuple-element.27), channel_id=1, source_target_pairs={{0,8},{8,16},{16,24},{1,9},{9,17},{17,25},{2,10},{10,18},{18,26},{... | collective-permute-start | bytes 1966088 | tf_op jit(solution)/shard_map/ppermute | solution.py:475
  32.4 0.0 copy-start.1
  32.4 0.0 copy-start.2
  32.4 0.0 copy-start.3
  32.4 0.0 copy-start.4
  32.4 1.4 %collective-permute-start.1 = (f32[5,32,8,128]{3,2,1,0:T(8,128)S(1)}, f32[5,32,8,128]{3,2,1,0:T(8,128)S(1)}, u32[]{:S(2)}, u32[]{:S(2)}) collective-permute-start(f32[5,32,8,128]{3,2,1,0:T(8,128)S(1)} %get-tuple-element.28), channel_id=1, source_target_pairs={{8,0},{16,8},{24,16},{9,1},{17,9},{25,17},{10,2},{18,10},{26,18},{... | collective-permute-start | bytes 1966088 | tf_op jit(solution)/shard_map/ppermute | solution.py:475
  33.8 2.1 %shard_map.67 = (f32[5,32,8,128]{3,2,1,0:T(8,128)S(1)}, f32[5,32,8,128]{3,2,1,0:T(8,128)S(1)}) custom-call(s32[1]{0:T(128)} %bitcast.me_ref, s32[32,1,48]{2,1,0:T(1,128)S(1)} %all-to-all-done.table, f32[24,5,32,8,128]{4,3,2,1,0:T(8,128)} %get-tuple-element.24.dense), custom_call_target="tpu_custom_call" | custom-call | tf_op jit(solution)/shard_map/pallas_call | solution.py:484
  36.0 2.8 %collective-permute-start.2 = (f32[5,32,8,128]{3,2,1,0:T(8,128)S(1)}, f32[5,32,8,128]{3,2,1,0:T(8,128)S(1)}, u32[]{:S(2)}, u32[]{:S(2)}) collective-permute-start(f32[5,32,8,128]{3,2,1,0:T(8,128)S(1)} %get-tuple-element.29), channel_id=1, source_target_pairs={{0,1},{1,2},{2,3},{3,4},{4,5},{5,6},{6,7},{8,9},{9,10},{10,11},{11... | collective-permute-start | bytes 1966088 | tf_op jit(solution)/shard_map/ppermute | solution.py:475
  38.8 0.0 collective-permute-done.4.f_xm
  38.8 1.3 %collective-permute-start.3 = (f32[5,32,8,128]{3,2,1,0:T(8,128)S(1)}, f32[5,32,8,128]{3,2,1,0:T(8,128)S(1)}, u32[]{:S(2)}, u32[]{:S(2)}) collective-permute-start(f32[5,32,8,128]{3,2,1,0:T(8,128)S(1)} %get-tuple-element.30), channel_id=1, source_target_pairs={{1,0},{2,1},{3,2},{4,3},{5,4},{6,5},{7,6},{9,8},{10,9},{11,10},{12... | collective-permute-start | bytes 1966088 | tf_op jit(solution)/shard_map/ppermute | solution.py:475
  40.1 0.0 collective-permute-done.5.f_xp
  40.1 5.3 %collective-permute-start.10 = (f32[6,5,8,128]{3,2,1,0:T(8,128)S(1)}, f32[6,5,8,128]{3,2,1,0:T(8,128)S(1)}, u32[]{:S(2)}, u32[]{:S(2)}) collective-permute-start(f32[6,5,8,128]{3,2,1,0:T(8,128)S(1)} %get-tuple-element.40), channel_id=1, source_target_pairs={{0,2},{1,3},{2,4},{3,5},{4,6},{5,7},{8,10},{9,11},{10,12},{11,13},... | collective-permute-start | bytes 368648 | tf_op jit(solution)/shard_map/ppermute | solution.py:475
  45.4 0.0 copy-done.1
  45.4 2.3 %shard_map.69 = (f32[12,5,8,128]{3,2,1,0:T(8,128)S(1)}, f32[12,5,8,128]{3,2,1,0:T(8,128)S(1)}) custom-call(s32[1]{0:T(128)} %bitcast.me_ref, s32[32,1,48]{2,1,0:T(1,128)S(1)} %all-to-all-done.table, f32[36,5,8,128]{3,2,1,0:T(8,128)S(1)} %copy-done.1, f32[36,5,8,128]{3,2,1,0:T(8,128)S(1)} %collective-permute-done.4.f_xm, ...), custom_call_target="tpu_custom_call" | custom-call | tf_op jit(solution)/shard_map/pallas_call | solution.py:484
  47.7 1.1 %collective-permute-done.10.g_y2m = f32[6,5,8,128]{3,2,1,0:T(8,128)S(1)} collective-permute-done((f32[6,5,8,128]{3,2,1,0:T(8,128)S(1)}, f32[6,5,8,128]{3,2,1,0:T(8,128)S(1)}, u32[]{:S(2)}, u32[]{:S(2)}) %collective-permute-start.10) | collective-permute-done | bytes 122912 | tf_op jit(solution)/shard_map/ppermute | solution.py:475
  48.8 10.6 %collective-permute-start.6 = (f32[12,5,8,128]{3,2,1,0:T(8,128)S(1)}, f32[12,5,8,128]{3,2,1,0:T(8,128)S(1)}, u32[]{:S(2)}, u32[]{:S(2)}) collective-permute-start(f32[12,5,8,128]{3,2,1,0:T(8,128)S(1)} %get-tuple-element.36), channel_id=1, source_target_pairs={{0,1},{1,2},{2,3},{3,4},{4,5},{5,6},{6,7},{8,9},{9,10},{10,11},{11... | collective-permute-start | bytes 737288 | tf_op jit(solution)/shard_map/ppermute | solution.py:475
  59.4 0.0 collective-permute-done.p_xm
  59.4 1.3 %collective-permute-start.7 = (f32[12,5,8,128]{3,2,1,0:T(8,128)S(1)}, f32[12,5,8,128]{3,2,1,0:T(8,128)S(1)}, u32[]{:S(2)}, u32[]{:S(2)}) collective-permute-start(f32[12,5,8,128]{3,2,1,0:T(8,128)S(1)} %get-tuple-element.37), channel_id=1, source_target_pairs={{1,0},{2,1},{3,2},{4,3},{5,4},{6,5},{7,6},{9,8},{10,9},{11,10},{12... | collective-permute-start | bytes 737288 | tf_op jit(solution)/shard_map/ppermute | solution.py:475
  60.7 0.0 collective-permute-done.1.p_xp
  60.7 1.3 %collective-permute-start.11 = (f32[6,5,8,128]{3,2,1,0:T(8,128)S(1)}, f32[6,5,8,128]{3,2,1,0:T(8,128)S(1)}, u32[]{:S(2)}, u32[]{:S(2)}) collective-permute-start(f32[6,5,8,128]{3,2,1,0:T(8,128)S(1)} %get-tuple-element.41), channel_id=1, source_target_pairs={{2,0},{3,1},{4,2},{5,3},{6,4},{7,5},{10,8},{11,9},{12,10},{13,11},... | collective-permute-start | bytes 368648 | tf_op jit(solution)/shard_map/ppermute | solution.py:475
  62.0 10.8 %collective-permute-done.2.p_ym = f32[5,32,8,128]{3,2,1,0:T(8,128)S(1)} collective-permute-done((f32[5,32,8,128]{3,2,1,0:T(8,128)S(1)}, f32[5,32,8,128]{3,2,1,0:T(8,128)S(1)}, u32[]{:S(2)}, u32[]{:S(2)}) %collective-permute-start.2) | collective-permute-done | bytes 655392 | tf_op jit(solution)/shard_map/ppermute | solution.py:475
  72.9 5.1 %collective-permute-start.8 = (f32[6,5,8,128]{3,2,1,0:T(8,128)S(1)}, f32[6,5,8,128]{3,2,1,0:T(8,128)S(1)}, u32[]{:S(2)}, u32[]{:S(2)}) collective-permute-start(f32[6,5,8,128]{3,2,1,0:T(8,128)S(1)} %get-tuple-element.38), channel_id=1, source_target_pairs={{0,16},{8,24},{1,17},{9,25},{2,18},{10,26},{3,19},{11,27},{4,20},{... | collective-permute-start | bytes 368648 | tf_op jit(solution)/shard_map/ppermute | solution.py:475
  77.9 0.0 collective-permute-done.3.p_yp
  77.9 1.3 %collective-permute-start.9 = (f32[6,5,8,128]{3,2,1,0:T(8,128)S(1)}, f32[6,5,8,128]{3,2,1,0:T(8,128)S(1)}, u32[]{:S(2)}, u32[]{:S(2)}) collective-permute-start(f32[6,5,8,128]{3,2,1,0:T(8,128)S(1)} %get-tuple-element.39), channel_id=1, source_target_pairs={{16,0},{24,8},{17,1},{25,9},{18,2},{26,10},{19,3},{27,11},{20,4},{... | collective-permute-start | bytes 368648 | tf_op jit(solution)/shard_map/ppermute | solution.py:475
  79.2 0.0 copy-done.2
  79.2 0.0 copy-done.3
  79.3 0.0 copy-done.4
  79.3 3.5 %shard_map.68 = (f32[2,5,520,128]{3,2,1,0:T(8,128)S(1)}, f32[2,5,32,8,128]{4,3,2,1,0:T(8,128)S(1)}, f32[2,5,32,8,128]{4,3,2,1,0:T(8,128)S(1)}, s32[2]{0:T(128)S(...) custom-call(s32[1]{0:T(128)} %bitcast.me_ref, s32[32,1,48]{2,1,0:T(1,128)S(1)} %all-to-all-done.table, f32[5]{0:T(128)S(1)} %copy-done.2, ...), custom_call_target="tpu_custom_call" | custom-call | tf_op jit(solution)/shard_map/pallas_call | solution.py:484
  82.7 0.0 collective-permute-done.11.g_y2p
  82.7 0.0 collective-permute-done.8.g_xm
  82.7 2.0 %collective-permute-done.9.g_xp = f32[6,5,8,128]{3,2,1,0:T(8,128)S(1)} collective-permute-done((f32[6,5,8,128]{3,2,1,0:T(8,128)S(1)}, f32[6,5,8,128]{3,2,1,0:T(8,128)S(1)}, u32[]{:S(2)}, u32[]{:S(2)}) %collective-permute-start.9) | collective-permute-done | bytes 122912 | tf_op jit(solution)/shard_map/ppermute | solution.py:475
  84.7 0.0 collective-permute-done.6.g_ym
  84.7 0.0 collective-permute-done.7.g_yp
  84.7 6.0 %shard_map.70 = f32[5,256,6,128]{3,2,1,0:T(8,128)} custom-call(s32[2]{0:T(128)S(1)} %get-tuple-element.31.patches, s32[24]{0:T(128)S(1)} %get-tuple-element.32.plan, f32[2,5,520,128]{3,2,1,0:T(8,128)S(1)} %get-tuple-element.33.grid, f32[2,5,32,8,128]{4,3,2,1,0:T(8,128)S(1)} %get-tuple-element.34.fixed, ...), custom_call_target="tpu_custom_call", output_to_operand_aliasing={{}: (14, {})} | custom-call | tf_op jit(solution)/shard_map/pallas_call | solution.py:484
Async XLA Ops:
  5.5 33.3 %collective-permute-start.4 = (f32[36,5,8,128]{3,2,1,0:T(8,128)}, f32[36,5,8,128]{3,2,1,0:T(8,128)S(1)}, u32[]{:S(2)}, u32[]{:S(2)}) collective-permute-start(f32[36,5,8,128]{3,2,1,0:T(8,128)} %get-tuple-element.25.faces.f_own), channel_id=1, source_target_pairs={{0,8},{8,16},{16,24},{1,9},{9,17},{17,25},{2,10},{10,18},{18,26},{... | collective-permute-start | bytes 2211848 | tf_op jit(solution)/shard_map/ppermute | solution.py:475
  7.9 32.1 %collective-permute-start.5 = (f32[36,5,8,128]{3,2,1,0:T(8,128)}, f32[36,5,8,128]{3,2,1,0:T(8,128)}, u32[]{:S(2)}, u32[]{:S(2)}) collective-permute-start(f32[36,5,8,128]{3,2,1,0:T(8,128)} %get-tuple-element.25.faces.f_own), channel_id=1, source_target_pairs={{8,0},{16,8},{24,16},{9,1},{17,9},{25,17},{10,2},{18,10},{26,18},{... | collective-permute-start | bytes 2211848 | tf_op jit(solution)/shard_map/ppermute | solution.py:475
  10.6 16.3 %all-to-all-start = ((s32[32,1,48]{2,1,0:T(1,128)}), s32[32,1,48]{2,1,0:T(1,128)S(1)}, u32[]{:S(2)}, u32[]{:S(2)}) async-start(s32[32,1,48]{2,1,0:T(1,128)} %shard_map.64), calls=%async_computation | async-start | bytes 32768 | tf_op jit(solution)/shard_map/all_to_all | solution.py:64
  26.9 1.1 %copy-start = (f32[36,5,8,128]{3,2,1,0:T(8,128)S(1)}, f32[36,5,8,128]{3,2,1,0:T(8,128)}, u32[]{:S(2)}) copy-start(f32[36,5,8,128]{3,2,1,0:T(8,128)} %get-tuple-element.25.faces.f_own) | copy-start | bytes 2211844
  30.6 28.9 %collective-permute-start = (f32[5,32,8,128]{3,2,1,0:T(8,128)S(1)}, f32[5,32,8,128]{3,2,1,0:T(8,128)S(1)}, u32[]{:S(2)}, u32[]{:S(2)}) collective-permute-start(f32[5,32,8,128]{3,2,1,0:T(8,128)S(1)} %get-tuple-element.27), channel_id=1, source_target_pairs={{0,8},{8,16},{16,24},{1,9},{9,17},{17,25},{2,10},{10,18},{18,26},{... | collective-permute-start | bytes 1966088 | tf_op jit(solution)/shard_map/ppermute | solution.py:475
  32.4 13.0 %copy-start.1 = (f32[36,5,8,128]{3,2,1,0:T(8,128)S(1)}, f32[36,5,8,128]{3,2,1,0:T(8,128)}, u32[]{:S(2)}) copy-start(f32[36,5,8,128]{3,2,1,0:T(8,128)} %get-tuple-element.25.faces.f_own) | copy-start | bytes 2211844
  32.4 46.9 %copy-start.2 = (f32[5]{0:T(128)S(1)}, f32[5]{0:T(128)}, u32[]{:S(2)}) copy-start(f32[5]{0:T(128)} %mob.1) | copy-start | bytes 64
  32.4 46.9 %copy-start.3 = (f32[5]{0:T(128)S(1)}, f32[5]{0:T(128)}, u32[]{:S(2)}) copy-start(f32[5]{0:T(128)} %gain.1) | copy-start | bytes 64
  32.4 46.9 %copy-start.4 = (f32[5]{0:T(128)S(1)}, f32[5]{0:T(128)}, u32[]{:S(2)}) copy-start(f32[5]{0:T(128)} %rates.1) | copy-start | bytes 64
  32.4 28.3 %collective-permute-start.1 = (f32[5,32,8,128]{3,2,1,0:T(8,128)S(1)}, f32[5,32,8,128]{3,2,1,0:T(8,128)S(1)}, u32[]{:S(2)}, u32[]{:S(2)}) collective-permute-start(f32[5,32,8,128]{3,2,1,0:T(8,128)S(1)} %get-tuple-element.28), channel_id=1, source_target_pairs={{8,0},{16,8},{24,16},{9,1},{17,9},{25,17},{10,2},{18,10},{26,18},{... | collective-permute-start | bytes 1966088 | tf_op jit(solution)/shard_map/ppermute | solution.py:475
  36.0 36.9 %collective-permute-start.2 = (f32[5,32,8,128]{3,2,1,0:T(8,128)S(1)}, f32[5,32,8,128]{3,2,1,0:T(8,128)S(1)}, u32[]{:S(2)}, u32[]{:S(2)}) collective-permute-start(f32[5,32,8,128]{3,2,1,0:T(8,128)S(1)} %get-tuple-element.29), channel_id=1, source_target_pairs={{0,1},{1,2},{2,3},{3,4},{4,5},{5,6},{6,7},{8,9},{9,10},{10,11},{11... | collective-permute-start | bytes 1966088 | tf_op jit(solution)/shard_map/ppermute | solution.py:475
  38.8 39.2 %collective-permute-start.3 = (f32[5,32,8,128]{3,2,1,0:T(8,128)S(1)}, f32[5,32,8,128]{3,2,1,0:T(8,128)S(1)}, u32[]{:S(2)}, u32[]{:S(2)}) collective-permute-start(f32[5,32,8,128]{3,2,1,0:T(8,128)S(1)} %get-tuple-element.30), channel_id=1, source_target_pairs={{1,0},{2,1},{3,2},{4,3},{5,4},{6,5},{7,6},{9,8},{10,9},{11,10},{12... | collective-permute-start | bytes 1966088 | tf_op jit(solution)/shard_map/ppermute | solution.py:475
  40.1 8.8 %collective-permute-start.10 = (f32[6,5,8,128]{3,2,1,0:T(8,128)S(1)}, f32[6,5,8,128]{3,2,1,0:T(8,128)S(1)}, u32[]{:S(2)}, u32[]{:S(2)}) collective-permute-start(f32[6,5,8,128]{3,2,1,0:T(8,128)S(1)} %get-tuple-element.40), channel_id=1, source_target_pairs={{0,2},{1,3},{2,4},{3,5},{4,6},{5,7},{8,10},{9,11},{10,12},{11,13},... | collective-permute-start | bytes 368648 | tf_op jit(solution)/shard_map/ppermute | solution.py:475
  48.8 35.9 %collective-permute-start.6 = (f32[12,5,8,128]{3,2,1,0:T(8,128)S(1)}, f32[12,5,8,128]{3,2,1,0:T(8,128)S(1)}, u32[]{:S(2)}, u32[]{:S(2)}) collective-permute-start(f32[12,5,8,128]{3,2,1,0:T(8,128)S(1)} %get-tuple-element.36), channel_id=1, source_target_pairs={{0,1},{1,2},{2,3},{3,4},{4,5},{5,6},{6,7},{8,9},{9,10},{10,11},{11... | collective-permute-start | bytes 737288 | tf_op jit(solution)/shard_map/ppermute | solution.py:475
  59.4 25.3 %collective-permute-start.7 = (f32[12,5,8,128]{3,2,1,0:T(8,128)S(1)}, f32[12,5,8,128]{3,2,1,0:T(8,128)S(1)}, u32[]{:S(2)}, u32[]{:S(2)}) collective-permute-start(f32[12,5,8,128]{3,2,1,0:T(8,128)S(1)} %get-tuple-element.37), channel_id=1, source_target_pairs={{1,0},{2,1},{3,2},{4,3},{5,4},{6,5},{7,6},{9,8},{10,9},{11,10},{12... | collective-permute-start | bytes 737288 | tf_op jit(solution)/shard_map/ppermute | solution.py:475
  60.7 22.0 %collective-permute-start.11 = (f32[6,5,8,128]{3,2,1,0:T(8,128)S(1)}, f32[6,5,8,128]{3,2,1,0:T(8,128)S(1)}, u32[]{:S(2)}, u32[]{:S(2)}) collective-permute-start(f32[6,5,8,128]{3,2,1,0:T(8,128)S(1)} %get-tuple-element.41), channel_id=1, source_target_pairs={{2,0},{3,1},{4,2},{5,3},{6,4},{7,5},{10,8},{11,9},{12,10},{13,11},... | collective-permute-start | bytes 368648 | tf_op jit(solution)/shard_map/ppermute | solution.py:475
  72.9 9.9 %collective-permute-start.8 = (f32[6,5,8,128]{3,2,1,0:T(8,128)S(1)}, f32[6,5,8,128]{3,2,1,0:T(8,128)S(1)}, u32[]{:S(2)}, u32[]{:S(2)}) collective-permute-start(f32[6,5,8,128]{3,2,1,0:T(8,128)S(1)} %get-tuple-element.38), channel_id=1, source_target_pairs={{0,16},{8,24},{1,17},{9,25},{2,18},{10,26},{3,19},{11,27},{4,20},{... | collective-permute-start | bytes 368648 | tf_op jit(solution)/shard_map/ppermute | solution.py:475
  77.9 6.8 %collective-permute-start.9 = (f32[6,5,8,128]{3,2,1,0:T(8,128)S(1)}, f32[6,5,8,128]{3,2,1,0:T(8,128)S(1)}, u32[]{:S(2)}, u32[]{:S(2)}) collective-permute-start(f32[6,5,8,128]{3,2,1,0:T(8,128)S(1)} %get-tuple-element.39), channel_id=1, source_target_pairs={{16,0},{24,8},{17,1},{25,9},{18,2},{26,10},{19,3},{27,11},{20,4},{... | collective-permute-start | bytes 368648 | tf_op jit(solution)/shard_map/ppermute | solution.py:475

commit v4 on v3

--- a/solution.py
+++ b/solution.py
@@ -134,11 +134,14 @@
         base = s * PER_S
 
         for p in range(cap):
+            for x in range(B):
+                dense[p, s, x] = rows[pl.ds(base + x * PER_X + p, TILES, stride=8), :]
+        copy_out(s).start()
+        for p in range(cap):
             start = base + p
             z_first = z_last = None
             for x in range(B):
-                v = rows[pl.ds(start + x * PER_X, TILES, stride=8), :]
-                dense[p, s, x] = v
+                v = dense[p, s, x]
                 a = v if x == 0 else pltpu.roll(v, x, 1)
                 b = v if x == B - 1 else pltpu.roll(v, 128 + x - (B - 1), 1)
                 z_first = a if x == 0 else jnp.where(z == x, a, z_first)
@@ -159,7 +162,6 @@
             faces[p * SIDES + 3, s] = y_last
             faces[p * SIDES + 4, s] = z_first
             faces[p * SIDES + 5, s] = z_last
-        copy_out(s).start()
         return carry
 
     lax.fori_loop(0, SPECIES, species, 0)

time: 91.4 us -> 91.4 us (level)
  no operation moved by 1% of the time
where the time goes in v4:
time: 91.4 us; the launch traced here: 90.7 us
  starting transfers between devices  45 us (49%)
  Pallas kernels  23.3 us (25%)
  waiting for transfers between devices  21.1 us (23%)
  local copies, waits for them, and re-layouts  1.14 us (1%)
    ppermute x12, starting transfers between devices, passed_along(): return lax.ppermute(x, axis, pairs)  35.8 us
    pallas_call x7, Pallas kernels, run(): pl.pallas_call(kernel, out_shape=out_shape, in_specs=in_specs, out_specs=...  23.3 us
    ppermute x12, waiting for transfers between devices, passed_along(): return lax.ppermute(x, axis, pairs)  13.9 us
    all_to_all x1, starting transfers between devices, gather(): return lax.all_to_all(sent, ('gx', 'gy'), 0, 0, tiled=True)  9.15 us
    all_to_all x1, waiting for transfers between devices, gather(): return lax.all_to_all(sent, ('gx', 'gy'), 0, 0, tiled=True)  7.13 us
  transfers between devices with their start and end apart: 13, of which 4 were waited for; matrix products, arithmetic and copies ran while one was open for 0% of the time, Pallas kernels for 13%

profile of v4, /device:TPU:0, one launch (start us, length us, event | category | flops | bytes accessed | tf_op | source)
XLA Modules:
  0.0 90.7 jit_solution(3896152852629584164)
XLA Ops:
  0.0 5.5 %shard_map.65 = (f32[24,5,32,8,128]{4,3,2,1,0:T(8,128)}, f32[36,5,8,128]{3,2,1,0:T(8,128)}) custom-call(f32[5,256,6,128]{3,2,1,0:T(8,128)} %bitcast.7), custom_call_target="tpu_custom_call" | custom-call | tf_op jit(solution)/shard_map/pallas_call | solution.py:486
  5.5 2.4 %collective-permute-start.4 = (f32[36,5,8,128]{3,2,1,0:T(8,128)}, f32[36,5,8,128]{3,2,1,0:T(8,128)S(1)}, u32[]{:S(2)}, u32[]{:S(2)}) collective-permute-start(f32[36,5,8,128]{3,2,1,0:T(8,128)} %get-tuple-element.25.faces.f_own), channel_id=1, source_target_pairs={{0,8},{8,16},{16,24},{1,9},{9,17},{17,25},{2,10},{10,18},{18,26},{... | collective-permute-start | bytes 2211848 | tf_op jit(solution)/shard_map/ppermute | solution.py:477
  7.9 1.3 %collective-permute-start.5 = (f32[36,5,8,128]{3,2,1,0:T(8,128)}, f32[36,5,8,128]{3,2,1,0:T(8,128)}, u32[]{:S(2)}, u32[]{:S(2)}) collective-permute-start(f32[36,5,8,128]{3,2,1,0:T(8,128)} %get-tuple-element.25.faces.f_own), channel_id=1, source_target_pairs={{8,0},{16,8},{24,16},{9,1},{17,9},{25,17},{10,2},{18,10},{26,18},{... | collective-permute-start | bytes 2211848 | tf_op jit(solution)/shard_map/ppermute | solution.py:477
  9.2 1.4 %shard_map.64 = s32[32,1,48]{2,1,0:T(1,128)} custom-call(s32[6]{0:T(128)} %source_slot.1, s32[6,6]{1,0:T(8,128)} %neighbours.1), custom_call_target="tpu_custom_call" | custom-call | tf_op jit(solution)/shard_map/pallas_call | solution.py:486
  10.6 9.2 %all-to-all-start = ((s32[32,1,48]{2,1,0:T(1,128)}), s32[32,1,48]{2,1,0:T(1,128)S(1)}, u32[]{:S(2)}, u32[]{:S(2)}) async-start(s32[32,1,48]{2,1,0:T(1,128)} %shard_map.64), calls=%async_computation | async-start | bytes 32768 | tf_op jit(solution)/shard_map/all_to_all | solution.py:64
  19.8 7.1 %all-to-all-done.table = s32[32,1,48]{2,1,0:T(1,128)S(1)} async-done(((s32[32,1,48]{2,1,0:T(1,128)}), s32[32,1,48]{2,1,0:T(1,128)S(1)}, u32[]{:S(2)}, u32[]{:S(2)}) %all-to-all-start) | async-done | bytes 6176 | tf_op jit(solution)/shard_map/all_to_all | solution.py:64
  26.9 0.0 copy-start
  26.9 1.1 %copy-done = f32[36,5,8,128]{3,2,1,0:T(8,128)S(1)} copy-done((f32[36,5,8,128]{3,2,1,0:T(8,128)S(1)}, f32[36,5,8,128]{3,2,1,0:T(8,128)}, u32[]{:S(2)}) %copy-start) | copy-done | bytes 737304
  28.0 2.5 %shard_map.66 = (f32[5,32,8,128]{3,2,1,0:T(8,128)S(1)}, f32[5,32,8,128]{3,2,1,0:T(8,128)S(1)}, f32[6,5,8,128]{3,2,1,0:T(8,128)S(1)}, f32[6,5,8,128]{3,2,1,0:T(8,...) custom-call(s32[1]{0:T(128)} %bitcast.me_ref, ...), custom_call_target="tpu_custom_call" | custom-call | tf_op jit(solution)/shard_map/pallas_call | solution.py:486
  30.5 1.8 %collective-permute-start = (f32[5,32,8,128]{3,2,1,0:T(8,128)S(1)}, f32[5,32,8,128]{3,2,1,0:T(8,128)S(1)}, u32[]{:S(2)}, u32[]{:S(2)}) collective-permute-start(f32[5,32,8,128]{3,2,1,0:T(8,128)S(1)} %get-tuple-element.27), channel_id=1, source_target_pairs={{0,8},{8,16},{16,24},{1,9},{9,17},{17,25},{2,10},{10,18},{18,26},{... | collective-permute-start | bytes 1966088 | tf_op jit(solution)/shard_map/ppermute | solution.py:477
  32.3 0.0 copy-start.1
  32.3 0.0 copy-start.2
  32.4 0.0 copy-start.3
  32.4 0.0 copy-start.4
  32.4 1.4 %collective-permute-start.1 = (f32[5,32,8,128]{3,2,1,0:T(8,128)S(1)}, f32[5,32,8,128]{3,2,1,0:T(8,128)S(1)}, u32[]{:S(2)}, u32[]{:S(2)}) collective-permute-start(f32[5,32,8,128]{3,2,1,0:T(8,128)S(1)} %get-tuple-element.28), channel_id=1, source_target_pairs={{8,0},{16,8},{24,16},{9,1},{17,9},{25,17},{10,2},{18,10},{26,18},{... | collective-permute-start | bytes 1966088 | tf_op jit(solution)/shard_map/ppermute | solution.py:477
  33.8 2.1 %shard_map.67 = (f32[5,32,8,128]{3,2,1,0:T(8,128)S(1)}, f32[5,32,8,128]{3,2,1,0:T(8,128)S(1)}) custom-call(s32[1]{0:T(128)} %bitcast.me_ref, s32[32,1,48]{2,1,0:T(1,128)S(1)} %all-to-all-done.table, f32[24,5,32,8,128]{4,3,2,1,0:T(8,128)} %get-tuple-element.24.dense), custom_call_target="tpu_custom_call" | custom-call | tf_op jit(solution)/shard_map/pallas_call | solution.py:486
  35.9 2.8 %collective-permute-start.2 = (f32[5,32,8,128]{3,2,1,0:T(8,128)S(1)}, f32[5,32,8,128]{3,2,1,0:T(8,128)S(1)}, u32[]{:S(2)}, u32[]{:S(2)}) collective-permute-start(f32[5,32,8,128]{3,2,1,0:T(8,128)S(1)} %get-tuple-element.29), channel_id=1, source_target_pairs={{0,1},{1,2},{2,3},{3,4},{4,5},{5,6},{6,7},{8,9},{9,10},{10,11},{11... | collective-permute-start | bytes 1966088 | tf_op jit(solution)/shard_map/ppermute | solution.py:477
  38.8 0.0 collective-permute-done.4.f_xm
  38.8 1.3 %collective-permute-start.3 = (f32[5,32,8,128]{3,2,1,0:T(8,128)S(1)}, f32[5,32,8,128]{3,2,1,0:T(8,128)S(1)}, u32[]{:S(2)}, u32[]{:S(2)}) collective-permute-start(f32[5,32,8,128]{3,2,1,0:T(8,128)S(1)} %get-tuple-element.30), channel_id=1, source_target_pairs={{1,0},{2,1},{3,2},{4,3},{5,4},{6,5},{7,6},{9,8},{10,9},{11,10},{12... | collective-permute-start | bytes 1966088 | tf_op jit(solution)/shard_map/ppermute | solution.py:477
  40.1 0.0 collective-permute-done.5.f_xp
  40.1 5.3 %collective-permute-start.10 = (f32[6,5,8,128]{3,2,1,0:T(8,128)S(1)}, f32[6,5,8,128]{3,2,1,0:T(8,128)S(1)}, u32[]{:S(2)}, u32[]{:S(2)}) collective-permute-start(f32[6,5,8,128]{3,2,1,0:T(8,128)S(1)} %get-tuple-element.40), channel_id=1, source_target_pairs={{0,2},{1,3},{2,4},{3,5},{4,6},{5,7},{8,10},{9,11},{10,12},{11,13},... | collective-permute-start | bytes 368648 | tf_op jit(solution)/shard_map/ppermute | solution.py:477
  45.4 0.0 copy-done.1
  45.4 2.3 %shard_map.69 = (f32[12,5,8,128]{3,2,1,0:T(8,128)S(1)}, f32[12,5,8,128]{3,2,1,0:T(8,128)S(1)}) custom-call(s32[1]{0:T(128)} %bitcast.me_ref, s32[32,1,48]{2,1,0:T(1,128)S(1)} %all-to-all-done.table, f32[36,5,8,128]{3,2,1,0:T(8,128)S(1)} %copy-done.1, f32[36,5,8,128]{3,2,1,0:T(8,128)S(1)} %collective-permute-done.4.f_xm, ...), custom_call_target="tpu_custom_call" | custom-call | tf_op jit(solution)/shard_map/pallas_call | solution.py:486
  47.7 1.1 %collective-permute-done.10.g_y2m = f32[6,5,8,128]{3,2,1,0:T(8,128)S(1)} collective-permute-done((f32[6,5,8,128]{3,2,1,0:T(8,128)S(1)}, f32[6,5,8,128]{3,2,1,0:T(8,128)S(1)}, u32[]{:S(2)}, u32[]{:S(2)}) %collective-permute-start.10) | collective-permute-done | bytes 122912 | tf_op jit(solution)/shard_map/ppermute | solution.py:477
  48.8 10.6 %collective-permute-start.6 = (f32[12,5,8,128]{3,2,1,0:T(8,128)S(1)}, f32[12,5,8,128]{3,2,1,0:T(8,128)S(1)}, u32[]{:S(2)}, u32[]{:S(2)}) collective-permute-start(f32[12,5,8,128]{3,2,1,0:T(8,128)S(1)} %get-tuple-element.36), channel_id=1, source_target_pairs={{0,1},{1,2},{2,3},{3,4},{4,5},{5,6},{6,7},{8,9},{9,10},{10,11},{11... | collective-permute-start | bytes 737288 | tf_op jit(solution)/shard_map/ppermute | solution.py:477
  59.4 0.0 collective-permute-done.p_xm
  59.4 1.3 %collective-permute-start.7 = (f32[12,5,8,128]{3,2,1,0:T(8,128)S(1)}, f32[12,5,8,128]{3,2,1,0:T(8,128)S(1)}, u32[]{:S(2)}, u32[]{:S(2)}) collective-permute-start(f32[12,5,8,128]{3,2,1,0:T(8,128)S(1)} %get-tuple-element.37), channel_id=1, source_target_pairs={{1,0},{2,1},{3,2},{4,3},{5,4},{6,5},{7,6},{9,8},{10,9},{11,10},{12... | collective-permute-start | bytes 737288 | tf_op jit(solution)/shard_map/ppermute | solution.py:477
  60.7 0.0 collective-permute-done.1.p_xp
  60.7 1.3 %collective-permute-start.11 = (f32[6,5,8,128]{3,2,1,0:T(8,128)S(1)}, f32[6,5,8,128]{3,2,1,0:T(8,128)S(1)}, u32[]{:S(2)}, u32[]{:S(2)}) collective-permute-start(f32[6,5,8,128]{3,2,1,0:T(8,128)S(1)} %get-tuple-element.41), channel_id=1, source_target_pairs={{2,0},{3,1},{4,2},{5,3},{6,4},{7,5},{10,8},{11,9},{12,10},{13,11},... | collective-permute-start | bytes 368648 | tf_op jit(solution)/shard_map/ppermute | solution.py:477
  62.0 10.8 %collective-permute-done.2.p_ym = f32[5,32,8,128]{3,2,1,0:T(8,128)S(1)} collective-permute-done((f32[5,32,8,128]{3,2,1,0:T(8,128)S(1)}, f32[5,32,8,128]{3,2,1,0:T(8,128)S(1)}, u32[]{:S(2)}, u32[]{:S(2)}) %collective-permute-start.2) | collective-permute-done | bytes 655392 | tf_op jit(solution)/shard_map/ppermute | solution.py:477
  72.8 5.1 %collective-permute-start.8 = (f32[6,5,8,128]{3,2,1,0:T(8,128)S(1)}, f32[6,5,8,128]{3,2,1,0:T(8,128)S(1)}, u32[]{:S(2)}, u32[]{:S(2)}) collective-permute-start(f32[6,5,8,128]{3,2,1,0:T(8,128)S(1)} %get-tuple-element.38), channel_id=1, source_target_pairs={{0,16},{8,24},{1,17},{9,25},{2,18},{10,26},{3,19},{11,27},{4,20},{... | collective-permute-start | bytes 368648 | tf_op jit(solution)/shard_map/ppermute | solution.py:477
  77.9 0.0 collective-permute-done.3.p_yp
  77.9 1.3 %collective-permute-start.9 = (f32[6,5,8,128]{3,2,1,0:T(8,128)S(1)}, f32[6,5,8,128]{3,2,1,0:T(8,128)S(1)}, u32[]{:S(2)}, u32[]{:S(2)}) collective-permute-start(f32[6,5,8,128]{3,2,1,0:T(8,128)S(1)} %get-tuple-element.39), channel_id=1, source_target_pairs={{16,0},{24,8},{17,1},{25,9},{18,2},{26,10},{19,3},{27,11},{20,4},{... | collective-permute-start | bytes 368648 | tf_op jit(solution)/shard_map/ppermute | solution.py:477
  79.2 0.0 copy-done.2
  79.2 0.0 copy-done.3
  79.2 0.0 copy-done.4
  79.3 3.5 %shard_map.68 = (f32[2,5,520,128]{3,2,1,0:T(8,128)S(1)}, f32[2,5,32,8,128]{4,3,2,1,0:T(8,128)S(1)}, f32[2,5,32,8,128]{4,3,2,1,0:T(8,128)S(1)}, s32[2]{0:T(128)S(...) custom-call(s32[1]{0:T(128)} %bitcast.me_ref, s32[32,1,48]{2,1,0:T(1,128)S(1)} %all-to-all-done.table, f32[5]{0:T(128)S(1)} %copy-done.2, ...), custom_call_target="tpu_custom_call" | custom-call | tf_op jit(solution)/shard_map/pallas_call | solution.py:486
  82.7 0.0 collective-permute-done.11.g_y2p
  82.7 0.0 collective-permute-done.8.g_xm
  82.7 2.0 %collective-permute-done.9.g_xp = f32[6,5,8,128]{3,2,1,0:T(8,128)S(1)} collective-permute-done((f32[6,5,8,128]{3,2,1,0:T(8,128)S(1)}, f32[6,5,8,128]{3,2,1,0:T(8,128)S(1)}, u32[]{:S(2)}, u32[]{:S(2)}) %collective-permute-start.9) | collective-permute-done | bytes 122912 | tf_op jit(solution)/shard_map/ppermute | solution.py:477
  84.7 0.0 collective-permute-done.6.g_ym
  84.7 0.0 collective-permute-done.7.g_yp
  84.7 6.0 %shard_map.70 = f32[5,256,6,128]{3,2,1,0:T(8,128)} custom-call(s32[2]{0:T(128)S(1)} %get-tuple-element.31.patches, s32[24]{0:T(128)S(1)} %get-tuple-element.32.plan, f32[2,5,520,128]{3,2,1,0:T(8,128)S(1)} %get-tuple-element.33.grid, f32[2,5,32,8,128]{4,3,2,1,0:T(8,128)S(1)} %get-tuple-element.34.fixed, ...), custom_call_target="tpu_custom_call", output_to_operand_aliasing={{}: (14, {})} | custom-call | tf_op jit(solution)/shard_map/pallas_call | solution.py:486
Async XLA Ops:
  5.5 33.3 %collective-permute-start.4 = (f32[36,5,8,128]{3,2,1,0:T(8,128)}, f32[36,5,8,128]{3,2,1,0:T(8,128)S(1)}, u32[]{:S(2)}, u32[]{:S(2)}) collective-permute-start(f32[36,5,8,128]{3,2,1,0:T(8,128)} %get-tuple-element.25.faces.f_own), channel_id=1, source_target_pairs={{0,8},{8,16},{16,24},{1,9},{9,17},{17,25},{2,10},{10,18},{18,26},{... | collective-permute-start | bytes 2211848 | tf_op jit(solution)/shard_map/ppermute | solution.py:477
  7.9 32.1 %collective-permute-start.5 = (f32[36,5,8,128]{3,2,1,0:T(8,128)}, f32[36,5,8,128]{3,2,1,0:T(8,128)}, u32[]{:S(2)}, u32[]{:S(2)}) collective-permute-start(f32[36,5,8,128]{3,2,1,0:T(8,128)} %get-tuple-element.25.faces.f_own), channel_id=1, source_target_pairs={{8,0},{16,8},{24,16},{9,1},{17,9},{25,17},{10,2},{18,10},{26,18},{... | collective-permute-start | bytes 2211848 | tf_op jit(solution)/shard_map/ppermute | solution.py:477
  10.6 16.3 %all-to-all-start = ((s32[32,1,48]{2,1,0:T(1,128)}), s32[32,1,48]{2,1,0:T(1,128)S(1)}, u32[]{:S(2)}, u32[]{:S(2)}) async-start(s32[32,1,48]{2,1,0:T(1,128)} %shard_map.64), calls=%async_computation | async-start | bytes 32768 | tf_op jit(solution)/shard_map/all_to_all | solution.py:64
  26.9 1.1 %copy-start = (f32[36,5,8,128]{3,2,1,0:T(8,128)S(1)}, f32[36,5,8,128]{3,2,1,0:T(8,128)}, u32[]{:S(2)}) copy-start(f32[36,5,8,128]{3,2,1,0:T(8,128)} %get-tuple-element.25.faces.f_own) | copy-start | bytes 2211844
  30.5 28.9 %collective-permute-start = (f32[5,32,8,128]{3,2,1,0:T(8,128)S(1)}, f32[5,32,8,128]{3,2,1,0:T(8,128)S(1)}, u32[]{:S(2)}, u32[]{:S(2)}) collective-permute-start(f32[5,32,8,128]{3,2,1,0:T(8,128)S(1)} %get-tuple-element.27), channel_id=1, source_target_pairs={{0,8},{8,16},{16,24},{1,9},{9,17},{17,25},{2,10},{10,18},{18,26},{... | collective-permute-start | bytes 1966088 | tf_op jit(solution)/shard_map/ppermute | solution.py:477
  32.3 13.0 %copy-start.1 = (f32[36,5,8,128]{3,2,1,0:T(8,128)S(1)}, f32[36,5,8,128]{3,2,1,0:T(8,128)}, u32[]{:S(2)}) copy-start(f32[36,5,8,128]{3,2,1,0:T(8,128)} %get-tuple-element.25.faces.f_own) | copy-start | bytes 2211844
  32.3 46.9 %copy-start.2 = (f32[5]{0:T(128)S(1)}, f32[5]{0:T(128)}, u32[]{:S(2)}) copy-start(f32[5]{0:T(128)} %mob.1) | copy-start | bytes 64
  32.4 46.9 %copy-start.3 = (f32[5]{0:T(128)S(1)}, f32[5]{0:T(128)}, u32[]{:S(2)}) copy-start(f32[5]{0:T(128)} %gain.1) | copy-start | bytes 64
  32.4 46.9 %copy-start.4 = (f32[5]{0:T(128)S(1)}, f32[5]{0:T(128)}, u32[]{:S(2)}) copy-start(f32[5]{0:T(128)} %rates.1) | copy-start | bytes 64
  32.4 28.3 %collective-permute-start.1 = (f32[5,32,8,128]{3,2,1,0:T(8,128)S(1)}, f32[5,32,8,128]{3,2,1,0:T(8,128)S(1)}, u32[]{:S(2)}, u32[]{:S(2)}) collective-permute-start(f32[5,32,8,128]{3,2,1,0:T(8,128)S(1)} %get-tuple-element.28), channel_id=1, source_target_pairs={{8,0},{16,8},{24,16},{9,1},{17,9},{25,17},{10,2},{18,10},{26,18},{... | collective-permute-start | bytes 1966088 | tf_op jit(solution)/shard_map/ppermute | solution.py:477
  35.9 36.9 %collective-permute-start.2 = (f32[5,32,8,128]{3,2,1,0:T(8,128)S(1)}, f32[5,32,8,128]{3,2,1,0:T(8,128)S(1)}, u32[]{:S(2)}, u32[]{:S(2)}) collective-permute-start(f32[5,32,8,128]{3,2,1,0:T(8,128)S(1)} %get-tuple-element.29), channel_id=1, source_target_pairs={{0,1},{1,2},{2,3},{3,4},{4,5},{5,6},{6,7},{8,9},{9,10},{10,11},{11... | collective-permute-start | bytes 1966088 | tf_op jit(solution)/shard_map/ppermute | solution.py:477
  38.8 39.2 %collective-permute-start.3 = (f32[5,32,8,128]{3,2,1,0:T(8,128)S(1)}, f32[5,32,8,128]{3,2,1,0:T(8,128)S(1)}, u32[]{:S(2)}, u32[]{:S(2)}) collective-permute-start(f32[5,32,8,128]{3,2,1,0:T(8,128)S(1)} %get-tuple-element.30), channel_id=1, source_target_pairs={{1,0},{2,1},{3,2},{4,3},{5,4},{6,5},{7,6},{9,8},{10,9},{11,10},{12... | collective-permute-start | bytes 1966088 | tf_op jit(solution)/shard_map/ppermute | solution.py:477
  40.1 8.8 %collective-permute-start.10 = (f32[6,5,8,128]{3,2,1,0:T(8,128)S(1)}, f32[6,5,8,128]{3,2,1,0:T(8,128)S(1)}, u32[]{:S(2)}, u32[]{:S(2)}) collective-permute-start(f32[6,5,8,128]{3,2,1,0:T(8,128)S(1)} %get-tuple-element.40), channel_id=1, source_target_pairs={{0,2},{1,3},{2,4},{3,5},{4,6},{5,7},{8,10},{9,11},{10,12},{11,13},... | collective-permute-start | bytes 368648 | tf_op jit(solution)/shard_map/ppermute | solution.py:477
  48.8 35.9 %collective-permute-start.6 = (f32[12,5,8,128]{3,2,1,0:T(8,128)S(1)}, f32[12,5,8,128]{3,2,1,0:T(8,128)S(1)}, u32[]{:S(2)}, u32[]{:S(2)}) collective-permute-start(f32[12,5,8,128]{3,2,1,0:T(8,128)S(1)} %get-tuple-element.36), channel_id=1, source_target_pairs={{0,1},{1,2},{2,3},{3,4},{4,5},{5,6},{6,7},{8,9},{9,10},{10,11},{11... | collective-permute-start | bytes 737288 | tf_op jit(solution)/shard_map/ppermute | solution.py:477
  59.4 25.3 %collective-permute-start.7 = (f32[12,5,8,128]{3,2,1,0:T(8,128)S(1)}, f32[12,5,8,128]{3,2,1,0:T(8,128)S(1)}, u32[]{:S(2)}, u32[]{:S(2)}) collective-permute-start(f32[12,5,8,128]{3,2,1,0:T(8,128)S(1)} %get-tuple-element.37), channel_id=1, source_target_pairs={{1,0},{2,1},{3,2},{4,3},{5,4},{6,5},{7,6},{9,8},{10,9},{11,10},{12... | collective-permute-start | bytes 737288 | tf_op jit(solution)/shard_map/ppermute | solution.py:477
  60.7 22.0 %collective-permute-start.11 = (f32[6,5,8,128]{3,2,1,0:T(8,128)S(1)}, f32[6,5,8,128]{3,2,1,0:T(8,128)S(1)}, u32[]{:S(2)}, u32[]{:S(2)}) collective-permute-start(f32[6,5,8,128]{3,2,1,0:T(8,128)S(1)} %get-tuple-element.41), channel_id=1, source_target_pairs={{2,0},{3,1},{4,2},{5,3},{6,4},{7,5},{10,8},{11,9},{12,10},{13,11},... | collective-permute-start | bytes 368648 | tf_op jit(solution)/shard_map/ppermute | solution.py:477
  72.8 9.9 %collective-permute-start.8 = (f32[6,5,8,128]{3,2,1,0:T(8,128)S(1)}, f32[6,5,8,128]{3,2,1,0:T(8,128)S(1)}, u32[]{:S(2)}, u32[]{:S(2)}) collective-permute-start(f32[6,5,8,128]{3,2,1,0:T(8,128)S(1)} %get-tuple-element.38), channel_id=1, source_target_pairs={{0,16},{8,24},{1,17},{9,25},{2,18},{10,26},{3,19},{11,27},{4,20},{... | collective-permute-start | bytes 368648 | tf_op jit(solution)/shard_map/ppermute | solution.py:477
  77.9 6.8 %collective-permute-start.9 = (f32[6,5,8,128]{3,2,1,0:T(8,128)S(1)}, f32[6,5,8,128]{3,2,1,0:T(8,128)S(1)}, u32[]{:S(2)}, u32[]{:S(2)}) collective-permute-start(f32[6,5,8,128]{3,2,1,0:T(8,128)S(1)} %get-tuple-element.39), channel_id=1, source_target_pairs={{16,0},{24,8},{17,1},{25,9},{18,2},{26,10},{19,3},{27,11},{20,4},{... | collective-permute-start | bytes 368648 | tf_op jit(solution)/shard_map/ppermute | solution.py:477
